TPU v7x, 32 devices: a whole 2x2x4 slice. The times are simulated.
32 devices in a mesh: dp: 4 (over x, y), tp: 8 (over z, core).
Axes of the slice: x: 2, y: 2, z: 4, core: 2. Of those that a mesh axis runs over, the one named last changes fastest.
Arguments:
- x: bfloat16 [13312, 2560], P(('dp', 'tp')), parts along dimension 0
- dy: bfloat16 [13312, 2560], P(('dp', 'tp')), parts along dimension 0
- pre: bfloat16 [13312, 10240], P('dp', 'tp'), parts along dimension 0
- w_in: bfloat16 [2560, 10240], P(None, 'tp')
- w_down: bfloat16 [10240, 2560], P('tp')
Outputs:
- output 1: bfloat16 [13312, 2560], P(('dp', 'tp')), parts along dimension 0
- output 2: bfloat16 [10240, 10240], P('dp', 'tp'), parts along dimension 0
- output 3: bfloat16 [40960, 2560], P(('dp', 'tp')), parts along dimension 0
There are 4 independent parts. A program takes and returns all parts, laid end to end along the dimension named above; an argument that names none is the same for every part.
All inputs are finite; a program needn't handle non-finite values.
Results may differ from a plain program's by a relative error of at most 0.012.
Values are sent between devices in bfloat16 or wider.
A program may use at most 2 GiB of HBM per device.

v0:
```python
import jax
import jax.numpy as jnp


def act(pre):
    return jax.nn.gelu(pre)


def solution(mesh):
    def step(x, dy, pre, w_in, w_down):
        hidden, back = jax.vjp(act, pre.astype(jnp.float32))
        d_hidden = jnp.dot(dy, w_down.T, preferred_element_type=jnp.float32)
        d_pre = back(d_hidden)[0].astype(jnp.bfloat16)
        dx = jnp.dot(d_pre, w_in.T)
        groups = mesh.shape["dp"]

        def by_group(a, b):
            a, b = (t.reshape(groups, -1, t.shape[-1]) for t in (a, b))
            product = jnp.einsum("gta,gtb->gab", a, b, preferred_element_type=jnp.float32)
            return product.astype(jnp.bfloat16).reshape(-1, b.shape[-1])

        return dx, by_group(x, d_pre), by_group(hidden.astype(jnp.bfloat16), dy)

    return step
```

profile of v0, /device:TPU:0, one launch (start us, length us, event | category | flops | bytes accessed | tf_op | source)
XLA Modules:
  0.0 497.8 jit_solution(504111473655839779)
XLA Ops:
  7.2 0.0 all-gather.10.cloned.1.call-start
  7.2 0.7 all-gather.10.cloned.1.call-update
  7.9 0.0 all-gather.12.cloned.1.call-start
  7.9 0.7 all-gather.12.cloned.1.call-update
  8.6 0.0 reduce-scatter.4.cloned.1.call-start
  8.7 156.8 %all-gather.10.cloned.1.call-done = bf16[3328,2560]{1,0:T(8,128)(2,1)} async-done(((bf16[416,2560]{1,0:T(8,128)(2,1)}), bf16[3328,2560]{1,0:T(8,128)(2,1)}) %all-gather.10.cloned.1.call-update) | async-done | bytes 17039376 | tf_op args[1]
  165.5 37.1 %fusion.3 = bf16[3328,1280]{1,0:T(8,128)(2,1)} fusion(bf16[3328,1280]{1,0:T(8,128)(2,1)} %param.2, bf16[3328,2560]{1,0:T(8,128)(2,1)} %all-gather.10.cloned.1.call-done, bf16[1280,2560]{1,0:T(8,128)(2,1)} %param.1), kind=kOutput, calls=%fused_computation.8 | convolution fusion | flops 21899837440 | bytes 40632320 | tf_op jit(solution)/dot_general | solution.py:12
  202.6 29.0 %fusion.20 = bf16[3328,2560]{1,0:T(8,128)(2,1)} fusion(bf16[3328,1280]{1,0:T(8,128)(2,1)} %fusion.3, bf16[2560,1280]{1,0:T(8,128)(2,1)} %param.3), kind=kOutput, calls=%fused_computation.26 | convolution fusion | flops 21810380800 | bytes 32112640 | tf_op jit(solution)/dot_general | solution.py:14
  231.6 0.0 reduce-scatter.4.cloned.1.call-update
  231.6 87.5 %all-gather.12.cloned.1.call-done = bf16[3328,2560]{1,0:T(8,128)(2,1)} async-done(((bf16[416,2560]{1,0:T(8,128)(2,1)}), bf16[3328,2560]{1,0:T(8,128)(2,1)}) %all-gather.12.cloned.1.call-update) | async-done | bytes 17039376 | tf_op jit(solution)/reshape | solution.py:18
  319.1 28.6 %fusion.10 = bf16[2560,1280]{0,1:T(8,128)(2,1)} fusion(bf16[3328,1280]{1,0:T(8,128)(2,1)} %fusion.3, bf16[3328,2560]{1,0:T(8,128)(2,1)} %all-gather.12.cloned.1.call-done), kind=kOutput, calls=%fused_computation.17 | convolution fusion | flops 21813657600 | bytes 32112640 | tf_op jit(solution)/gta,gtb->gab/dot_general | solution.py:19
  347.8 9.5 %copy = bf16[2560,1280]{1,0:T(8,128)(2,1)} copy(bf16[2560,1280]{0,1:T(8,128)(2,1)} %fusion.10) | data formatting | bytes 13107200
  357.2 35.9 %convolution_convert_fusion = bf16[1280,2560]{1,0:T(8,128)(2,1)} fusion(bf16[3328,2560]{1,0:T(8,128)(2,1)} %all-gather.10.cloned.1.call-done, bf16[3328,1280]{1,0:T(8,128)(2,1)} %param.2), kind=kOutput, calls=%fused_computation.15 | convolution fusion | flops 21856256000 | bytes 32112640 | tf_op jit(solution)/gta,gtb->gab/dot_general | solution.py:19
  393.1 98.2 %reduce-scatter.4.cloned.1.call-done = bf16[416,2560]{1,0:T(8,128)(2,1)} async-done(((bf16[3328,2560]{1,0:T(8,128)(2,1)}), bf16[416,2560]{1,0:T(8,128)(2,1)}) %reduce-scatter.4.cloned.1.call-update) | async-done | bytes 2129936
Async XLA Ops:
  7.2 158.4 %all-gather.10.cloned.1.call-start = ((), (), s32[]{:S(2)}) async-start(), calls=%async_computation.1 | async-start | bytes 19169280 | tf_op args[1]
  7.9 311.2 %all-gather.12.cloned.1.call-start = ((), (), s32[]{:S(2)}) async-start(), calls=%async_computation.2 | async-start | bytes 19169280 | tf_op jit(solution)/reshape | solution.py:18
  8.6 482.6 %reduce-scatter.4.cloned.1.call-start = ((), (), s32[]{:S(2)}) async-start(), calls=%async_computation.3 | async-start | bytes 19169280
Sparse Core Ops, SparseCore 0:
  9.6 155.8 all-gather.9
  167.2 151.8 all-gather.11
  322.1 169.1 reduce-scatter.3
where the time goes:
time: 498 us
  waiting for transfers between devices  344 us (69%)
  matrix products  131 us (26%)
  between operations  13.7 us (3%)
  local copies, waits for them, and re-layouts  9.48 us (2%)
    unnamed x5, waiting for transfers between devices  256 us
    reshape x1, waiting for transfers between devices, by_group(): a, b = (t.reshape(groups, -1, t.shape[-1]) for t in (a, b))  87.5 us
    dot_general x2, matrix products, by_group(): jnp.einsum('gta,gtb->gab', a, b, preferred_element_type=jnp.float32)  64.5 us
    dot_general x1, matrix products, step(): d_hidden = jnp.dot(dy, w_down.T, preferred_element_type=jnp.float32)  37.1 us
    dot_general x1, matrix products, step(): dx = jnp.dot(d_pre, w_in.T)  29 us
  transfers between devices with their start and end apart: 3, of which 3 were waited for; matrix products, arithmetic and copies ran while one was open for 28% of the time, Pallas kernels for 0%

commit v1 on v0

v1 whole, which is shorter than its diff:
```python
import functools

import jax
import jax.numpy as jnp
from jax import lax
from jax.experimental import pallas as pl
from jax.experimental.pallas import tpu as pltpu
from jax.sharding import PartitionSpec as P

Z = 4
NT = (((1,), (1,)), ((), ()))
TN = (((0,), (0,)), ((), ()))
F32, BF16 = jnp.float32, jnp.bfloat16
K0 = 0.7978845608028654
K1 = 0.044715
TILE = 256


def gelu_and_slope(p):
    p2 = p * p
    t = jnp.tanh(K0 * (p + K1 * (p * p2)))
    cdf = 0.5 * (1.0 + t)
    slope = cdf + (0.5 * p) * (1.0 - t * t) * (K0 * (1.0 + (3.0 * K1) * p2))
    return p * cdf, slope


def line_kernel(
    x_ref, dy_ref, pre_ref, wi_ref, wd_ref,
    xg, dyg, dpre_o, dwd_o, base_o, last_o, rin, pin, rout,
    wi, wd, acc, dp, dyb, preb, hid, pxb, pv, rv, sb, bb,
    ssem, rsem, ps, pr, pxs, pxr, rs_s, rs_r, lsem,
):
    B, D = dy_ref.shape
    H = B // 2
    F = wd_ref.shape[0]
    PAD = dyb.shape[0]
    tp = lax.axis_index("tp")
    z, c = tp // 2, tp % 2
    partner = z * 2 + (1 - c)
    arrs, gathered = (dy_ref, x_ref), (dyg, xg)
    sign = (1, -1)
    place = (z, Z - 1 - z)
    ahead = tuple(jnp.clip(tp + 2 * s, 0, 2 * Z - 1) for s in sign)

    def remote(src, dst, send, recv, to):
        return pltpu.make_async_remote_copy(
            src_ref=src, dst_ref=dst, send_sem=send, recv_sem=recv,
            device_id={"tp": to}, device_id_type=pl.DeviceIdType.MESH,
        )

    def local(src, dst, i):
        return pltpu.make_async_copy(src, dst, lsem.at[i])

    def sync(src, dst, i):
        cp = local(src, dst, i)
        cp.start()
        cp.wait()

    def rows_of(chip, core, h):
        return pl.ds(pl.multiple_of((chip * 2 + core) * B + h * H, 16), H)

    def block_of(chip, core):
        return pl.ds(pl.multiple_of((chip * 2 + core) * B, 32), B)

    def half(h):
        return pl.ds(pl.multiple_of(h * H, 16), H)

    barrier = pltpu.get_barrier_semaphore()
    pl.semaphore_signal(barrier, inc=1, device_id={"tp": partner}, device_id_type=pl.DeviceIdType.MESH)
    for d in (0, 1):
        @pl.when(place[d] < Z - 1)
        def _():
            pl.semaphore_signal(barrier, inc=1, device_id={"tp": ahead[d]}, device_id_type=pl.DeviceIdType.MESH)
    pl.semaphore_wait(barrier, jnp.where((z > 0) & (z < Z - 1), 3, 2))

    def own_send(d, a, h):
        return remote(arrs[a].at[half(h)], gathered[a].at[rows_of(z, c, h)],
                      ssem.at[d, a, 0, h], rsem.at[d, a, 0, h], ahead[d])

    def line_send(d, a, s, h):
        r = rows_of(z - sign[d] * s, c, h)
        return remote(gathered[a].at[r], gathered[a].at[r],
                      ssem.at[d, a, s, h], rsem.at[d, a, s, h], ahead[d])

    def line_arrival(d, a, s, h):
        r = rows_of(z - sign[d] * s, c, h)
        return remote(gathered[a].at[r], gathered[a].at[r],
                      ssem.at[d, a, 0, h], rsem.at[d, a, s - 1, h], ahead[d])

    def own_to_partner(a, h):
        return remote(arrs[a].at[half(h)], gathered[a].at[rows_of(z, c, h)],
                      ps.at[a, z, h], pr.at[a, z, h], partner)

    def to_partner(a, chip, h):
        r = rows_of(chip, c, h)
        return remote(gathered[a].at[r], gathered[a].at[r],
                      ps.at[a, chip, h], pr.at[a, chip, h], partner)

    def from_partner(a, chip, h):
        r = rows_of(chip, 1 - c, h)
        return remote(gathered[a].at[r], gathered[a].at[r],
                      ps.at[a, chip, h], pr.at[a, chip, h], partner)

    for h in (0, 1):
        for d in (0, 1):
            @pl.when(place[d] < Z - 1)
            def _():
                own_send(d, 0, h).start()
    for h in (0, 1):
        own_to_partner(0, h).start()
    local(wd_ref, wd, 6).start()
    local(wi_ref, wi, 7).start()
    for h in (0, 1):
        own_to_partner(1, h).start()

    dyb[pl.ds(B, PAD - B), :] = jnp.zeros((PAD - B, D), BF16)
    hid[pl.ds(B, PAD - B), :] = jnp.zeros((PAD - B, F), BF16)

    def zero(i, _):
        acc[pl.ds(pl.multiple_of(i * 64, 64), 64), :] = jnp.zeros((64, D), F32)
        return 0

    lax.fori_loop(0, F // 64, zero, 0)
    local(wd_ref, wd, 6).wait()
    local(wi_ref, wi, 7).wait()

    def arrive(d, a, s, h):
        line_arrival(d, a, s, h).wait_recv()

        @pl.when(place[d] < Z - 1)
        def _():
            line_send(d, a, s, h).start()
        to_partner(a, z - sign[d] * s, h).start()

    def chip_at(k):
        outer = (z == 0) | (z == Z - 1)
        o = jnp.where(outer, k, jnp.where(k < 2, 1 - k, k))
        return jnp.where(z < 2, o, Z - 1 - o)

    def px_send(chip, k):
        return remote(pxb, pin.at[chip], pxs.at[k], pxr.at[chip], partner)

    def cols(n, width=TILE):
        return pl.ds(pl.multiple_of(n * width, width), width)

    def slot(t, _):
        s, h = (t + 1) // 2, (t + 1) % 2
        for d in (0, 1):
            q = place[d]

            @pl.when((t >= 1) & (s <= q))
            def _():
                arrive(d, 0, s, h)

            @pl.when((t >= 1) & (s > q) & (s <= 2 * q))
            def _():
                arrive(d, 1, s - q, h)

            @pl.when((t == 2 * q) & (q < Z - 1))
            def _():
                for hh in (0, 1):
                    own_send(d, 1, hh).start()

        def rs(j, _):
            outer = (z == 0) | (z == Z - 1)
            u0, u1 = jnp.maximum(t - 4, 0), jnp.maximum(t - 7, 0)
            k = jnp.where(outer, (u0 // 2 + 1) % 4, jnp.where(j == 0, (u1 // 2 + 2) % 4, 1))
            b = jnp.where(z < 2, k, Z - 1 - k)
            hh = jnp.where(outer, u0 % 2, jnp.where(j == 0, u1 % 2, (t + 1) % 2))
            first = jnp.where(outer, 4, jnp.where(j == 0, 7, 9))
            end = jnp.where(outer, jnp.where(j == 0, 12, 0), jnp.where(j == 0, 13, 11))

            @pl.when((t >= first) & (t < end))
            def _():
                inner = (z > 0) & (z < Z - 1)
                has = (inner & (b >= z), inner & (b <= z))

                @pl.when(hh == 0)
                def _():
                    remote(pxb, pin.at[b], pxs.at[0], pxr.at[b], partner).wait_recv()
                local(pin.at[b, half(hh)], pv, 0).start()
                for d in (0, 1):
                    @pl.when(has[d])
                    def _():
                        remote(rin.at[d, b, half(hh)], rin.at[d, b, half(hh)],
                               rs_s.at[b, hh], rs_r.at[d, b, hh], partner).wait_recv()
                        local(rin.at[d, b, half(hh)], rv.at[d], 1 + d).start()

                    @pl.when(jnp.logical_not(has[d]))
                    def _():
                        rv[d] = jnp.zeros(rv.shape[1:], BF16)
                local(pin.at[b, half(hh)], pv, 0).wait()
                for d in (0, 1):
                    @pl.when(has[d])
                    def _():
                        local(rin.at[d, b, half(hh)], rv.at[d], 1 + d).wait()

                def tile(n, _):
                    cs = cols(n)
                    g = lax.dot_general(dp[rows_of(b, c, hh), :], wi[cs, :], NT, preferred_element_type=F32)
                    g = g + pv[:, cs].astype(F32)
                    g = g + (rv[0, :, cs].astype(F32) + rv[1, :, cs].astype(F32))
                    bb[:, cs] = g
                    sb[:, cs] = g.astype(BF16)
                    return 0

                lax.fori_loop(0, D // TILE, tile, 0)
                to_last = ((z == 1) & (b == 0)) | ((z == Z - 2) & (b == Z - 1))

                @pl.when(b == z)
                def _():
                    sync(bb, base_o.at[half(hh)], 3)

                @pl.when(to_last)
                def _():
                    sync(sb, last_o.at[half(hh)], 3)

                @pl.when((b != z) & jnp.logical_not(to_last))
                def _():
                    sync(sb, rout.at[b, half(hh)], 3)
                    for d in (0, 1):
                        @pl.when((b > z) if d == 0 else (b < z))
                        def _():
                            r_send(d, b, hh).start()
            return 0

        def r_send(d, b, hh):
            return remote(rout.at[b, half(hh)], rin.at[d, b, half(hh)],
                          rs_s.at[b, hh], rs_r.at[d, b, hh], ahead[d])

        lax.fori_loop(0, 2, rs, 0)

        @pl.when(t < 8)
        def _():
            k = t // 2
            chip = chip_at(k)
            odd = t % 2
            core = jnp.where(odd == 0, c, 1 - c)
            blk = block_of(chip, core)
            local(pre_ref.at[blk], preb, 0).start()

            @pl.when(odd == 1)
            def _():
                for hh in (0, 1):
                    from_partner(0, chip, hh).wait_recv()

            @pl.when(t == 0)
            def _():
                sync(dy_ref, dyb.at[pl.ds(0, B)], 1)

            @pl.when(t > 0)
            def _():
                sync(dyg.at[blk], dyb.at[pl.ds(0, B)], 1)
            local(pre_ref.at[blk], preb, 0).wait()

            def t1(n, _):
                cs = cols(n)
                g = lax.dot_general(dyb[pl.ds(0, B), :], wd[cs, :], NT, preferred_element_type=F32)
                hidden, slope = gelu_and_slope(preb[:, cs].astype(F32))
                hid[pl.ds(0, B), cs] = hidden.astype(BF16)
                dp[blk, cs] = (g * slope).astype(BF16)
                return 0

            lax.fori_loop(0, F // TILE, t1, 0)

            @pl.when(odd == 1)
            def _():
                @pl.when(k > 0)
                def _():
                    px_send(chip, k - 1).wait_send()

                def px(n, _):
                    cs = cols(n)
                    g = lax.dot_general(dp[blk, :], wi[cs, :], NT, preferred_element_type=F32)
                    pxb[:, cs] = g.astype(BF16)
                    return 0

                lax.fori_loop(0, D // TILE, px, 0)
                px_send(chip, k).start()

            def t2(m, _):
                ms = cols(m)
                acc[ms, :] += lax.dot_general(hid[:, ms], dyb[...], TN, preferred_element_type=F32)
                return 0

            lax.fori_loop(0, F // TILE, t2, 0)

        @pl.when(t == 8)
        def _():
            local(dp, dpre_o, 4).start()
            sync(x_ref, dyb.at[pl.ds(0, B)], 1)
            sync(dyb.at[pl.ds(0, B)], xg.at[block_of(z, c)], 1)

            def flush(m, _):
                ms = cols(m)
                dyb[pl.ds(0, TILE), :] = acc[ms, :].astype(BF16)
                sync(dyb.at[pl.ds(0, TILE)], dwd_o.at[ms], 1)
                return 0

            lax.fori_loop(0, F // TILE, flush, 0)
        return 0

    lax.fori_loop(0, 13, slot, 0)

    local(dp, dpre_o, 4).wait()
    px_send(0, 3).wait_send()
    for chip in range(Z):
        for h in (0, 1):
            for a in (0, 1):
                to_partner(a, chip, h).wait_send()
            from_partner(1, chip, h).wait_recv()
            kept = ((z == 1) & (chip == 0)) | ((z == Z - 2) & (chip == Z - 1))

            @pl.when((z != chip) & jnp.logical_not(kept))
            def _():
                remote(rout.at[chip, half(h)], rin.at[0, chip, half(h)],
                       rs_s.at[chip, h], rs_r.at[0, chip, h], partner).wait_send()
    for d in (0, 1):
        for s in range(Z - 1):
            @pl.when((place[d] < Z - 1) & (s <= place[d]))
            def _():
                for a in (0, 1):
                    for h in (0, 1):
                        line_send(d, a, s, h).wait_send()


def line_step(x, dy, pre, w_in, w_down):
    B, D = dy.shape
    H = B // 2
    R, F = pre.shape
    PAD = -(-B // TILE) * TILE
    hbm = pl.BlockSpec(memory_space=pltpu.HBM)
    sds = jax.ShapeDtypeStruct
    dma = pltpu.SemaphoreType.DMA
    return pl.pallas_call(
        line_kernel,
        out_shape=[
            sds((R, D), BF16), sds((R, D), BF16), sds((R, F), BF16), sds((F, D), BF16),
            sds((B, D), F32), sds((B, D), BF16),
            sds((2, Z, B, D), BF16), sds((Z, B, D), BF16), sds((Z, B, D), BF16),
        ],
        in_specs=[hbm] * 5,
        out_specs=[hbm] * 9,
        scratch_shapes=[
            pltpu.VMEM((D, F), BF16), pltpu.VMEM((F, D), BF16), pltpu.VMEM((F, D), F32),
            pltpu.VMEM((R, F), BF16), pltpu.VMEM((PAD, D), BF16), pltpu.VMEM((B, F), BF16),
            pltpu.VMEM((PAD, F), BF16), pltpu.VMEM((B, D), BF16), pltpu.VMEM((H, D), BF16),
            pltpu.VMEM((2, H, D), BF16), pltpu.VMEM((H, D), BF16), pltpu.VMEM((H, D), F32),
            dma((2, 2, 3, 2)), dma((2, 2, 3, 2)), dma((2, Z, 2)), dma((2, Z, 2)),
            dma((Z,)), dma((Z,)), dma((Z, 2)), dma((2, Z, 2)), dma((8,)),
        ],
        compiler_params=pltpu.CompilerParams(
            collective_id=0, has_side_effects=True, vmem_limit_bytes=62 * 1024 * 1024
        ),
        cost_estimate=pl.CostEstimate(flops=6 * R * D * F, bytes_accessed=12 * R * D, transcendentals=R * F),
    )(x, dy, pre, w_in, w_down)


def dw_kernel(a_ref, b_ref, o_ref):
    o_ref[...] = lax.dot_general(a_ref[...], b_ref[...], TN, preferred_element_type=F32).astype(o_ref.dtype)


def weight_grad(a, b, width=512):
    R, D = a.shape
    F = b.shape[1]
    return pl.pallas_call(
        dw_kernel,
        grid=(D // width,),
        out_shape=jax.ShapeDtypeStruct((D, F), BF16),
        in_specs=[pl.BlockSpec((R, width), lambda i: (0, i)), pl.BlockSpec((R, F), lambda i: (0, 0))],
        out_specs=pl.BlockSpec((width, F), lambda i: (i, 0)),
        compiler_params=pltpu.CompilerParams(vmem_limit_bytes=48 * 1024 * 1024),
        cost_estimate=pl.CostEstimate(flops=2 * R * D * F, bytes_accessed=2 * (R * D + R * F + D * F), transcendentals=0),
    )(a, b)


def solution(mesh):
    def body(x, dy, pre, w_in, w_down):
        xg, _, d_pre, dw_down, base, last, _, _, _ = line_step(x, dy, pre, w_in, w_down)
        hops = [(2 + c, c) for c in (0, 1)] + [(2 * Z - 4 + c, 2 * Z - 2 + c) for c in (0, 1)]
        came = lax.ppermute(last, "tp", hops)
        dw_in = weight_grad(xg, d_pre)
        dx = (base + came.astype(F32)).astype(BF16)
        return dx, dw_in, dw_down

    rows = P(("dp", "tp"), None)
    return jax.shard_map(
        body, mesh=mesh,
        in_specs=(rows, rows, P("dp", "tp"), P(None, "tp"), P("tp", None)),
        out_specs=(rows, P("dp", "tp"), rows),
        check_vma=False,
    )
```

time: 498 us -> 341 us (0.68)
  waiting for transfers between devices: 344 us -> 22.1 us
  Pallas kernels: 0 us -> 311 us
  matrix products: 131 us -> 0 us
  between operations: 13.7 us -> 0.67 us
  local copies, waits for them, and re-layouts: 9.48 us -> 2.8 us
    pallas_call x0 -> x2, Pallas kernels: none -> 311 us  [the longest x1 282 us: line_step(): pl.pallas_call(line_kernel, out_shape=[sds((R, D), BF16), sds((R, D), BF1...]
    unnamed x5 -> x0, waiting for transfers between devices: 256 us -> none
    dot_general x4 -> x0, matrix products: 131 us -> none  [the longest x2 64.5 us: by_group(): jnp.einsum('gta,gtb->gab', a, b, preferred_element_type=jnp.float32)]
    reshape x1 -> x0, waiting for transfers between devices: 87.5 us -> none  [by_group(): a, b = (t.reshape(groups, -1, t.shape[-1]) for t in (a, b))]
    ppermute x0 -> x1, waiting for transfers between devices: none -> 22.1 us  [body(): came = lax.ppermute(last, 'tp', hops)]
    unnamed x1 -> x7, local copies, waits for them, and re-layouts: 9.48 us -> 2.8 us
  transfers between devices with their start and end apart: 3 -> 1, of which waited for: 3 -> 1; matrix products, arithmetic and copies ran while one was open for 28% -> 0% of each run, Pallas kernels for 0% -> 8%
where the time goes in v1:
time: 341 us; the launch traced here: 340 us
  Pallas kernels  311 us (91%)
  waiting for transfers between devices  22.1 us (6%)
    pallas_call x1, Pallas kernels, line_step(): pl.pallas_call(line_kernel, out_shape=[sds((R, D), BF16), sds((R, D), BF1...  282 us
    pallas_call x1, Pallas kernels, weight_grad(): pl.pallas_call(dw_kernel, grid=(D // width,), out_shape=jax.ShapeDtypeStr...  28.8 us
    ppermute x1, waiting for transfers between devices, body(): came = lax.ppermute(last, 'tp', hops)  22.1 us
  transfers between devices with their start and end apart: 1, of which 1 were waited for; matrix products, arithmetic and copies ran while one was open for 0% of the time, Pallas kernels for 8%

profile of v1, /device:TPU:0, one launch (start us, length us, event | category | flops | bytes accessed | tf_op | source)
XLA Modules:
  0.0 340.0 jit_solution(15832604534858334884)
XLA Ops:
  0.6 282.4 %shard_map.76 = (bf16[3328,2560]{1,0:T(8,128)(2,1)}, bf16[3328,2560]{1,0:T(8,128)(2,1)}, bf16[3328,1280]{1,0:T(8,128)(2,1)}, bf16[1280,2560]{1,0:T(8,128)(2,1)},...) custom-call(bf16[416,2560]{1,0:T(8,128)(2,1)} %x_ref.1, ...), custom_call_target="tpu_custom_call" | custom-call | flops 65431142400 | bytes 102236160 | tf_op jit(solution)/shard_map/pallas_call | solution.py:335
  283.0 1.3 collective-permute-start
  284.3 0.0 slice-start
  284.3 0.0 copy-start
  284.3 0.0 slice-start.1
  284.4 28.8 %shard_map.77 = bf16[2560,1280]{1,0:T(8,128)(2,1)} custom-call(bf16[3328,2560]{1,0:T(8,128)(2,1)} %get-tuple-element.10.a_ref, bf16[3328,1280]{1,0:T(8,128)(2,1)} %get-tuple-element.11.b_ref), custom_call_target="tpu_custom_call" | custom-call | flops 21810380800 | bytes 32112640 | tf_op jit(solution)/shard_map/pallas_call | solution.py:366
  313.1 22.1 %collective-permute-done = bf16[416,2560]{1,0:T(8,128)(2,1)S(1)} collective-permute-done((bf16[416,2560]{1,0:T(8,128)(2,1)}, bf16[416,2560]{1,0:T(8,128)(2,1)S(1)}, u32[]{:S(2)}, u32[]{:S(2)}) %collective-permute-start) | collective-permute-done | bytes 2129952 | tf_op jit(solution)/shard_map/ppermute | solution.py:381
  335.2 0.0 copy-done
  335.2 2.0 add_convert_fusion
  337.2 0.0 slice-done
  337.2 0.0 slice-done.1
  337.2 2.8 copy.9
  (1 shorter events, 0.0 us)
Async XLA Ops:
  283.0 52.2 %collective-permute-start = (bf16[416,2560]{1,0:T(8,128)(2,1)}, bf16[416,2560]{1,0:T(8,128)(2,1)S(1)}, u32[]{:S(2)}, u32[]{:S(2)}) collective-permute-start(bf16[416,2560]{1,0:T(8,128)(2,1)} %get-tuple-element.9), channel_id=1, source_target_pairs={{2,0},{3,1},{4,6},{5,7},{10,8},{11,9},{12,14},{13,15},{18,16},{19,... | collective-permute-start | bytes 6389768 | tf_op jit(solution)/shard_map/ppermute | solution.py:381
  284.3 52.8 %slice-start = ((s8[6553600]{0:T(1024)(128)(4,1)}), s8[4194304]{0:T(1024)(128)(4,1)S(1)}, s32[]{:S(2)}) async-start(s8[6553600]{0:T(1024)(128)(4,1)} %bitcast), calls=%async_computation | async-start | bytes 8388608
  284.3 50.9 %copy-start = (f32[416,2560]{1,0:T(8,128)S(1)}, f32[416,2560]{1,0:T(8,128)}, u32[]{:S(2)}) copy-start(f32[416,2560]{1,0:T(8,128)} %get-tuple-element.8) | copy-start | bytes 12779524
  284.3 52.8 %slice-start.1 = ((s8[6553600]{0:T(1024)(128)(4,1)}), s8[2359296]{0:T(1024)(128)(4,1)S(1)}, s32[]{:S(2)}) async-start(s8[6553600]{0:T(1024)(128)(4,1)} %bitcast), calls=%async_computation.1 | async-start | bytes 4718592

commit v2 on v1

--- a/solution.py
+++ b/solution.py
@@ -26,7 +26,7 @@
 
 def line_kernel(
     x_ref, dy_ref, pre_ref, wi_ref, wd_ref,
-    xg, dyg, dpre_o, dwd_o, base_o, last_o, rin, pin, rout,
+    xg, dyg, dpre_o, dwd_o, part_o, base_o, late_base_o, last_o, came_o, rin, pin, rout,
     wi, wd, acc, dp, dyb, preb, hid, pxb, pv, rv, sb, bb,
     ssem, rsem, ps, pr, pxs, pxr, rs_s, rs_r, lsem,
 ):
@@ -56,11 +56,26 @@
         cp.start()
         cp.wait()
 
+    def turn(zz, k):
+        outer = (zz == 0) | (zz == Z - 1)
+        o = jnp.where(outer, k, jnp.where(k < 2, 1 - k, k))
+        return jnp.where(zz < 2, o, Z - 1 - o)
+
+    def spot(a, zz, chip):
+        if a == 0:
+            return chip
+        p = jnp.where(zz < 2, chip, Z - 1 - chip)
+        outer = (zz == 0) | (zz == Z - 1)
+        return jnp.where(outer, p, jnp.where(p < 2, 1 - p, p))
+
     def rows_of(chip, core, h):
         return pl.ds(pl.multiple_of((chip * 2 + core) * B + h * H, 16), H)
 
     def block_of(chip, core):
         return pl.ds(pl.multiple_of((chip * 2 + core) * B, 32), B)
+
+    def chip_rows(chip):
+        return pl.ds(pl.multiple_of(chip * 2 * B, 64), 2 * B)
 
     def half(h):
         return pl.ds(pl.multiple_of(h * H, 16), H)
@@ -74,30 +89,31 @@
     pl.semaphore_wait(barrier, jnp.where((z > 0) & (z < Z - 1), 3, 2))
 
     def own_send(d, a, h):
-        return remote(arrs[a].at[half(h)], gathered[a].at[rows_of(z, c, h)],
+        return remote(arrs[a].at[half(h)], gathered[a].at[rows_of(spot(a, z + sign[d], z), c, h)],
                       ssem.at[d, a, 0, h], rsem.at[d, a, 0, h], ahead[d])
 
     def line_send(d, a, s, h):
-        r = rows_of(z - sign[d] * s, c, h)
-        return remote(gathered[a].at[r], gathered[a].at[r],
+        chip = z - sign[d] * s
+        return remote(gathered[a].at[rows_of(spot(a, z, chip), c, h)],
+                      gathered[a].at[rows_of(spot(a, z + sign[d], chip), c, h)],
                       ssem.at[d, a, s, h], rsem.at[d, a, s, h], ahead[d])
 
     def line_arrival(d, a, s, h):
-        r = rows_of(z - sign[d] * s, c, h)
+        r = rows_of(spot(a, z, z - sign[d] * s), c, h)
         return remote(gathered[a].at[r], gathered[a].at[r],
                       ssem.at[d, a, 0, h], rsem.at[d, a, s - 1, h], ahead[d])
 
     def own_to_partner(a, h):
-        return remote(arrs[a].at[half(h)], gathered[a].at[rows_of(z, c, h)],
+        return remote(arrs[a].at[half(h)], gathered[a].at[rows_of(spot(a, z, z), c, h)],
                       ps.at[a, z, h], pr.at[a, z, h], partner)
 
     def to_partner(a, chip, h):
-        r = rows_of(chip, c, h)
+        r = rows_of(spot(a, z, chip), c, h)
         return remote(gathered[a].at[r], gathered[a].at[r],
                       ps.at[a, chip, h], pr.at[a, chip, h], partner)
 
     def from_partner(a, chip, h):
-        r = rows_of(chip, 1 - c, h)
+        r = rows_of(spot(a, z, chip), 1 - c, h)
         return remote(gathered[a].at[r], gathered[a].at[r],
                       ps.at[a, chip, h], pr.at[a, chip, h], partner)
 
@@ -131,11 +147,6 @@
         def _():
             line_send(d, a, s, h).start()
         to_partner(a, z - sign[d] * s, h).start()
-
-    def chip_at(k):
-        outer = (z == 0) | (z == Z - 1)
-        o = jnp.where(outer, k, jnp.where(k < 2, 1 - k, k))
-        return jnp.where(z < 2, o, Z - 1 - o)
 
     def px_send(chip, k):
         return remote(pxb, pin.at[chip], pxs.at[k], pxr.at[chip], partner)
@@ -205,35 +216,51 @@
                     return 0
 
                 lax.fori_loop(0, D // TILE, tile, 0)
-                to_last = ((z == 1) & (b == 0)) | ((z == Z - 2) & (b == Z - 1))
+                to_end = ((z == 1) & (b == 0)) | ((z == Z - 2) & (b == Z - 1))
+                to_last = to_end & (hh == 1)
 
                 @pl.when(b == z)
                 def _():
-                    sync(bb, base_o.at[half(hh)], 3)
+                    @pl.when(hh == 0)
+                    def _():
+                        sync(bb, base_o, 3)
+
+                    @pl.when(hh == 1)
+                    def _():
+                        sync(bb, late_base_o, 3)
 
                 @pl.when(to_last)
                 def _():
-                    sync(sb, last_o.at[half(hh)], 3)
+                    sync(sb, last_o, 3)
 
                 @pl.when((b != z) & jnp.logical_not(to_last))
                 def _():
                     sync(sb, rout.at[b, half(hh)], 3)
                     for d in (0, 1):
-                        @pl.when((b > z) if d == 0 else (b < z))
+                        goes = (b > z) if d == 0 else (b < z)
+
+                        @pl.when(goes & jnp.logical_not(to_end))
                         def _():
                             r_send(d, b, hh).start()
+
+                        @pl.when(goes & to_end)
+                        def _():
+                            end_send(d, b).start()
             return 0
 
         def r_send(d, b, hh):
             return remote(rout.at[b, half(hh)], rin.at[d, b, half(hh)],
                           rs_s.at[b, hh], rs_r.at[d, b, hh], ahead[d])
 
+        def end_send(d, b):
+            return remote(rout.at[b, half(0)], came_o, rs_s.at[b, 0], rs_r.at[d, b, 0], ahead[d])
+
         lax.fori_loop(0, 2, rs, 0)
 
         @pl.when(t < 8)
         def _():
             k = t // 2
-            chip = chip_at(k)
+            chip = turn(z, k)
             odd = t % 2
             core = jnp.where(odd == 0, c, 1 - c)
             blk = block_of(chip, core)
@@ -287,41 +314,77 @@
 
         @pl.when(t == 8)
         def _():
-            local(dp, dpre_o, 4).start()
+            for k in (2, 3):
+                local(dp.at[chip_rows(turn(z, k))], dpre_o.at[pl.ds((k - 2) * 2 * B, 2 * B)], 2 + k).start()
+
+            @pl.when((z > 0) & (z < Z - 1))
+            def _():
+                pv[...] = jnp.zeros(pv.shape, BF16)
+                sync(pv, came_o, 1)
             sync(x_ref, dyb.at[pl.ds(0, B)], 1)
-            sync(dyb.at[pl.ds(0, B)], xg.at[block_of(z, c)], 1)
+            sync(dyb.at[pl.ds(0, B)], xg.at[block_of(spot(1, z, z), c)], 1)
 
             def flush(m, _):
                 ms = cols(m)
                 dyb[pl.ds(0, TILE), :] = acc[ms, :].astype(BF16)
+                acc[ms, :] = jnp.zeros((TILE, D), F32)
                 sync(dyb.at[pl.ds(0, TILE)], dwd_o.at[ms], 1)
                 return 0
 
             lax.fori_loop(0, F // TILE, flush, 0)
+
+        @pl.when(t >= 9)
+        def _():
+            k = (t - 9) // 2
+            odd = (t - 9) % 2
+            chip = turn(z, k)
+            core = jnp.where(odd == 0, c, 1 - c)
+
+            @pl.when(odd == 1)
+            def _():
+                for hh in (0, 1):
+                    from_partner(1, chip, hh).wait_recv()
+            sync(xg.at[block_of(k, core)], dyb.at[pl.ds(0, B)], 1)
+
+            def t4(m, _):
+                for i in (0, 1):
+                    acc[cols(m), pl.ds(i * F, F)] += lax.dot_general(
+                        dyb[pl.ds(0, B), cols(2 * m + i)], dp[block_of(chip, core), :], TN,
+                        preferred_element_type=F32)
+                return 0
+
+            lax.fori_loop(0, D // (2 * TILE), t4, 0)
         return 0
 
     lax.fori_loop(0, 13, slot, 0)
 
-    local(dp, dpre_o, 4).wait()
+    local(acc, part_o, 1).start()
+    for k in (2, 3):
+        local(dp.at[pl.ds(0, 2 * B)], dpre_o.at[pl.ds(0, 2 * B)], 2 + k).wait()
+        for h in (0, 1):
+            from_partner(1, turn(z, k), h).wait_recv()
     px_send(0, 3).wait_send()
     for chip in range(Z):
         for h in (0, 1):
             for a in (0, 1):
                 to_partner(a, chip, h).wait_send()
-            from_partner(1, chip, h).wait_recv()
             kept = ((z == 1) & (chip == 0)) | ((z == Z - 2) & (chip == Z - 1))
 
-            @pl.when((z != chip) & jnp.logical_not(kept))
+            @pl.when((z != chip) & (jnp.logical_not(kept) if h else (z < Z)))
             def _():
                 remote(rout.at[chip, half(h)], rin.at[0, chip, half(h)],
                        rs_s.at[chip, h], rs_r.at[0, chip, h], partner).wait_send()
     for d in (0, 1):
+        @pl.when(place[d] == Z - 1)
+        def _():
+            remote(came_o, came_o, rs_s.at[0, 0], rs_r.at[d, z, 0], partner).wait_recv()
         for s in range(Z - 1):
             @pl.when((place[d] < Z - 1) & (s <= place[d]))
             def _():
                 for a in (0, 1):
                     for h in (0, 1):
                         line_send(d, a, s, h).wait_send()
+    local(acc, part_o, 1).wait()
 
 
 def line_step(x, dy, pre, w_in, w_down):
@@ -335,12 +398,12 @@
     return pl.pallas_call(
         line_kernel,
         out_shape=[
-            sds((R, D), BF16), sds((R, D), BF16), sds((R, F), BF16), sds((F, D), BF16),
-            sds((B, D), F32), sds((B, D), BF16),
+            sds((R, D), BF16), sds((R, D), BF16), sds((R // 2, F), BF16), sds((F, D), BF16), sds((F, D), F32),
+            sds((H, D), F32), sds((H, D), F32), sds((H, D), BF16), sds((H, D), BF16),
             sds((2, Z, B, D), BF16), sds((Z, B, D), BF16), sds((Z, B, D), BF16),
         ],
         in_specs=[hbm] * 5,
-        out_specs=[hbm] * 9,
+        out_specs=[hbm] * 12,
         scratch_shapes=[
             pltpu.VMEM((D, F), BF16), pltpu.VMEM((F, D), BF16), pltpu.VMEM((F, D), F32),
             pltpu.VMEM((R, F), BF16), pltpu.VMEM((PAD, D), BF16), pltpu.VMEM((B, F), BF16),
@@ -356,31 +419,46 @@
     )(x, dy, pre, w_in, w_down)
 
 
-def dw_kernel(a_ref, b_ref, o_ref):
-    o_ref[...] = lax.dot_general(a_ref[...], b_ref[...], TN, preferred_element_type=F32).astype(o_ref.dtype)
-
-
-def weight_grad(a, b, width=512):
-    R, D = a.shape
-    F = b.shape[1]
+def finish_kernel(a_ref, b_ref, part_ref, w_ref, base_ref, came_ref, o_ref, wo_ref, dx_ref):
+    rows, width = part_ref.shape[0], b_ref.shape[1]
+    for i in (0, 1):
+        band = pl.ds(i * rows, rows)
+        g = lax.dot_general(a_ref[:, band], b_ref[...], TN, preferred_element_type=F32)
+        o_ref[band, :] = (part_ref[:, pl.ds(i * width, width)] + g).astype(o_ref.dtype)
+    wo_ref[...] = w_ref[...]
+
+    @pl.when(pl.program_id(0) == 0)
+    def _():
+        dx_ref[...] = (base_ref[...] + came_ref[...].astype(F32)).astype(dx_ref.dtype)
+
+
+def finish(x, d_pre, part, dw_down, base, came):
+    D = x.shape[1]
+    R, F = d_pre.shape
+    n = D // (2 * TILE)
+    H = came.shape[0]
+    sds = jax.ShapeDtypeStruct
+    first = pl.BlockSpec((H, D), lambda i: (0, 0))
+    band = pl.BlockSpec((F // n, D), lambda i: (i, 0))
     return pl.pallas_call(
-        dw_kernel,
-        grid=(D // width,),
-        out_shape=jax.ShapeDtypeStruct((D, F), BF16),
-        in_specs=[pl.BlockSpec((R, width), lambda i: (0, i)), pl.BlockSpec((R, F), lambda i: (0, 0))],
-        out_specs=pl.BlockSpec((width, F), lambda i: (i, 0)),
-        compiler_params=pltpu.CompilerParams(vmem_limit_bytes=48 * 1024 * 1024),
-        cost_estimate=pl.CostEstimate(flops=2 * R * D * F, bytes_accessed=2 * (R * D + R * F + D * F), transcendentals=0),
-    )(a, b)
+        finish_kernel,
+        grid=(n,),
+        out_shape=[sds((D, F), BF16), sds((F, D), BF16), sds((2 * H, D), BF16)],
+        in_specs=[pl.BlockSpec((R, D // n), lambda i: (1, i)), pl.BlockSpec((R, F), lambda i: (0, 0)),
+                  band, band, first, first],
+        out_specs=[pl.BlockSpec((D // n, F), lambda i: (i, 0)), band, first],
+        compiler_params=pltpu.CompilerParams(vmem_limit_bytes=56 * 1024 * 1024),
+        cost_estimate=pl.CostEstimate(flops=2 * R * D * F, bytes_accessed=2 * (R * D + R * F + 5 * D * F), transcendentals=0),
+    )(x, d_pre, part, dw_down, base, came)
 
 
 def solution(mesh):
     def body(x, dy, pre, w_in, w_down):
-        xg, _, d_pre, dw_down, base, last, _, _, _ = line_step(x, dy, pre, w_in, w_down)
+        xg, _, d_pre, dw_down, part, base, late_base, last, came, _, _, _ = line_step(x, dy, pre, w_in, w_down)
         hops = [(2 + c, c) for c in (0, 1)] + [(2 * Z - 4 + c, 2 * Z - 2 + c) for c in (0, 1)]
-        came = lax.ppermute(last, "tp", hops)
-        dw_in = weight_grad(xg, d_pre)
-        dx = (base + came.astype(F32)).astype(BF16)
+        late = lax.ppermute(last, "tp", hops)
+        dw_in, dw_down, dx = finish(xg, d_pre, part, dw_down, base, came)
+        dx = lax.dynamic_update_slice(dx, (late_base + late.astype(F32)).astype(BF16), (came.shape[0], 0))
         return dx, dw_in, dw_down
 
     rows = P(("dp", "tp"), None)

time: 341 us -> 332 us (0.974)
  waiting for transfers between devices: 22.1 us -> 2.23 us
  Pallas kernels: 311 us -> 326 us
    pallas_call x1, Pallas kernels: 282 us -> 303 us  [line_step(): pl.pallas_call(line_kernel, out_shape=[sds((R, D), BF16), sds((R, D), BF1...]
    ppermute x1, waiting for transfers between devices: 22.1 us -> 2.23 us  [body(): late = lax.ppermute(last, 'tp', hops)]
    pallas_call x1, Pallas kernels: 28.8 us -> 22.9 us  [finish(): pl.pallas_call(finish_kernel, grid=(n,), out_shape=[sds((D, F), BF16), sd...]
  transfers between devices with their start and end apart: 1 -> 1, of which waited for: 1 -> 1; matrix products, arithmetic and copies ran while one was open for 0% -> 0% of each run, Pallas kernels for 8% -> 7%
where the time goes in v2:
time: 332 us; the launch traced here: 331 us
  Pallas kernels  326 us (98%)
    pallas_call x1, Pallas kernels, line_step(): pl.pallas_call(line_kernel, out_shape=[sds((R, D), BF16), sds((R, D), BF1...  303 us
    pallas_call x1, Pallas kernels, finish(): pl.pallas_call(finish_kernel, grid=(n,), out_shape=[sds((D, F), BF16), sd...  22.9 us
  transfers between devices with their start and end apart: 1, of which 1 were waited for; matrix products, arithmetic and copies ran while one was open for 0% of the time, Pallas kernels for 7%

profile of v2, /device:TPU:0, one launch (start us, length us, event | category | flops | bytes accessed | tf_op | source)
XLA Modules:
  0.0 331.1 jit_solution(1862914252805866279)
XLA Ops:
  0.6 302.9 %shard_map.76 = (bf16[3328,2560]{1,0:T(8,128)(2,1)}, bf16[3328,2560]{1,0:T(8,128)(2,1)}, bf16[1664,1280]{1,0:T(8,128)(2,1)}, bf16[1280,2560]{1,0:T(8,128)(2,1)},...) custom-call(bf16[416,2560]{1,0:T(8,128)(2,1)} %x_ref.1, ...), custom_call_target="tpu_custom_call" | custom-call | flops 65431142400 | bytes 102236160 | tf_op jit(solution)/shard_map/pallas_call | solution.py:398
  303.5 1.3 collective-permute-start
  304.8 0.0 copy-start
  304.8 22.9 %shard_map.77 = (bf16[2560,1280]{1,0:T(8,128)(2,1)}, bf16[1280,2560]{1,0:T(8,128)(2,1)}, bf16[416,2560]{1,0:T(8,128)(2,1)}) custom-call(bf16[3328,2560]{1,0:T(8,128)(2,1)} %get-tuple-element.14.a_ref, bf16[1664,1280]{1,0:T(8,128)(2,1)} %get-tuple-element.15.b_ref, f32[1280,2560]{1,0:T(8,128)} %get-tuple-element.16.part_ref, ...), custom_call_target="tpu_custom_call" | custom-call | flops 10905190400 | bytes 45547520 | tf_op jit(solution)/shard_map/pallas_call | solution.py:443
  327.7 2.2 collective-permute-done
  329.9 0.0 copy-done
  329.9 1.2 fusion
Async XLA Ops:
  303.5 26.4 %collective-permute-start = (bf16[208,2560]{1,0:T(8,128)(2,1)}, bf16[208,2560]{1,0:T(8,128)(2,1)S(1)}, u32[]{:S(2)}, u32[]{:S(2)}) collective-permute-start(bf16[208,2560]{1,0:T(8,128)(2,1)} %get-tuple-element.22), channel_id=1, source_target_pairs={{2,0},{3,1},{4,6},{5,7},{10,8},{11,9},{12,14},{13,15},{18,16},{19,... | collective-permute-start | bytes 3194888 | tf_op jit(solution)/shard_map/ppermute | solution.py:459
  304.8 25.1 %copy-start = (f32[208,2560]{1,0:T(8,128)S(1)}, f32[208,2560]{1,0:T(8,128)}, u32[]{:S(2)}) copy-start(f32[208,2560]{1,0:T(8,128)} %get-tuple-element.21) | copy-start | bytes 6389764

commit v3 on v2

--- a/solution.py
+++ b/solution.py
@@ -14,6 +14,7 @@
 K0 = 0.7978845608028654
 K1 = 0.044715
 TILE = 256
+EARLY, MID = 32, 160
 
 
 def gelu_and_slope(p):
@@ -26,7 +27,7 @@
 
 def line_kernel(
     x_ref, dy_ref, pre_ref, wi_ref, wd_ref,
-    xg, dyg, dpre_o, dwd_o, part_o, base_o, late_base_o, last_o, came_o, rin, pin, rout,
+    xg, dyg, dpre_o, dwd_o, part_o, base_o, late_base_o, mid_o, last_o, came_o, rin, pin, rout,
     wi, wd, acc, dp, dyb, preb, hid, pxb, pv, rv, sb, bb,
     ssem, rsem, ps, pr, pxs, pxr, rs_s, rs_r, lsem,
 ):
@@ -34,6 +35,8 @@
     H = B // 2
     F = wd_ref.shape[0]
     PAD = dyb.shape[0]
+    early, mid = EARLY, MID
+    rest = H - early - mid
     tp = lax.axis_index("tp")
     z, c = tp // 2, tp % 2
     partner = z * 2 + (1 - c)
@@ -151,6 +154,12 @@
     def px_send(chip, k):
         return remote(pxb, pin.at[chip], pxs.at[k], pxr.at[chip], partner)
 
+    def end_send(d, b):
+        return remote(rout.at[b, pl.ds(0, early)], came_o.at[pl.ds(0, early)], rs_s.at[b, 0], rs_r.at[d, b, 0], ahead[d])
+
+    def mid_send(d, b):
+        return remote(mid_o, came_o.at[pl.ds(early, mid)], rs_s.at[b, 1], rs_r.at[d, b, 1], ahead[d])
+
     def cols(n, width=TILE):
         return pl.ds(pl.multiple_of(n * width, width), width)
 
@@ -171,6 +180,10 @@
             def _():
                 for hh in (0, 1):
                     own_send(d, 1, hh).start()
+
+        @pl.when(t == 12)
+        def _():
+            local(acc, part_o, 6).start()
 
         def rs(j, _):
             outer = (z == 0) | (z == Z - 1)
@@ -217,43 +230,49 @@
 
                 lax.fori_loop(0, D // TILE, tile, 0)
                 to_end = ((z == 1) & (b == 0)) | ((z == Z - 2) & (b == Z - 1))
-                to_last = to_end & (hh == 1)
-
                 @pl.when(b == z)
                 def _():
                     @pl.when(hh == 0)
                     def _():
-                        sync(bb, base_o, 3)
+                        sync(bb.at[pl.ds(0, early + mid)], base_o, 3)
+                        sync(bb.at[pl.ds(early + mid, rest)], late_base_o.at[pl.ds(0, rest)], 3)
 
                     @pl.when(hh == 1)
                     def _():
-                        sync(bb, late_base_o, 3)
-
-                @pl.when(to_last)
+                        sync(bb, late_base_o.at[pl.ds(rest, H)], 3)
+
+                @pl.when(to_end)
                 def _():
-                    sync(sb, last_o, 3)
-
-                @pl.when((b != z) & jnp.logical_not(to_last))
+                    @pl.when(hh == 0)
+                    def _():
+                        sync(sb.at[pl.ds(0, early)], rout.at[b, pl.ds(0, early)], 3)
+                        sync(sb.at[pl.ds(early, mid)], mid_o, 3)
+                        for d in (0, 1):
+                            @pl.when((b > z) if d == 0 else (b < z))
+                            def _():
+                                end_send(d, b).start()
+
+                                @pl.when(c == 1)
+                                def _():
+                                    mid_send(d, b).start()
+                        sync(sb.at[pl.ds(early + mid, rest)], last_o.at[pl.ds(0, rest)], 3)
+
+                    @pl.when(hh == 1)
+                    def _():
+                        sync(sb, last_o.at[pl.ds(rest, H)], 3)
+
+                @pl.when((b != z) & jnp.logical_not(to_end))
                 def _():
                     sync(sb, rout.at[b, half(hh)], 3)
                     for d in (0, 1):
-                        goes = (b > z) if d == 0 else (b < z)
-
-                        @pl.when(goes & jnp.logical_not(to_end))
+                        @pl.when((b > z) if d == 0 else (b < z))
                         def _():
                             r_send(d, b, hh).start()
-
-                        @pl.when(goes & to_end)
-                        def _():
-                            end_send(d, b).start()
             return 0
 
         def r_send(d, b, hh):
             return remote(rout.at[b, half(hh)], rin.at[d, b, half(hh)],
                           rs_s.at[b, hh], rs_r.at[d, b, hh], ahead[d])
-
-        def end_send(d, b):
-            return remote(rout.at[b, half(0)], came_o, rs_s.at[b, 0], rs_r.at[d, b, 0], ahead[d])
 
         lax.fori_loop(0, 2, rs, 0)
 
@@ -317,10 +336,15 @@
             for k in (2, 3):
                 local(dp.at[chip_rows(turn(z, k))], dpre_o.at[pl.ds((k - 2) * 2 * B, 2 * B)], 2 + k).start()
 
+            pv[...] = jnp.zeros(pv.shape, BF16)
+
+            @pl.when(((z > 0) & (z < Z - 1)) | (c == 0))
+            def _():
+                sync(pv.at[pl.ds(0, mid)], came_o.at[pl.ds(early, mid)], 1)
+
             @pl.when((z > 0) & (z < Z - 1))
             def _():
-                pv[...] = jnp.zeros(pv.shape, BF16)
-                sync(pv, came_o, 1)
+                sync(pv.at[pl.ds(0, early)], came_o.at[pl.ds(0, early)], 1)
             sync(x_ref, dyb.at[pl.ds(0, B)], 1)
             sync(dyb.at[pl.ds(0, B)], xg.at[block_of(spot(1, z, z), c)], 1)
 
@@ -333,10 +357,10 @@
 
             lax.fori_loop(0, F // TILE, flush, 0)
 
-        @pl.when(t >= 9)
-        def _():
-            k = (t - 9) // 2
-            odd = (t - 9) % 2
+        @pl.when((t >= 8) & (t < 12))
+        def _():
+            k = (t - 8) // 2
+            odd = t % 2
             chip = turn(z, k)
             core = jnp.where(odd == 0, c, 1 - c)
 
@@ -358,7 +382,6 @@
 
     lax.fori_loop(0, 13, slot, 0)
 
-    local(acc, part_o, 1).start()
     for k in (2, 3):
         local(dp.at[pl.ds(0, 2 * B)], dpre_o.at[pl.ds(0, 2 * B)], 2 + k).wait()
         for h in (0, 1):
@@ -370,21 +393,30 @@
                 to_partner(a, chip, h).wait_send()
             kept = ((z == 1) & (chip == 0)) | ((z == Z - 2) & (chip == Z - 1))
 
-            @pl.when((z != chip) & (jnp.logical_not(kept) if h else (z < Z)))
+            @pl.when(kept & ((h == 0) | (c == 1)))
+            def _():
+                (mid_send if h else end_send)(0, chip).wait_send()
+
+            @pl.when((z != chip) & jnp.logical_not(kept))
             def _():
                 remote(rout.at[chip, half(h)], rin.at[0, chip, half(h)],
                        rs_s.at[chip, h], rs_r.at[0, chip, h], partner).wait_send()
     for d in (0, 1):
         @pl.when(place[d] == Z - 1)
         def _():
-            remote(came_o, came_o, rs_s.at[0, 0], rs_r.at[d, z, 0], partner).wait_recv()
+            end_send(d, z).wait_recv()
+
+            @pl.when(c == 1)
+            def _():
+                mid_send(d, z).wait_recv()
+
         for s in range(Z - 1):
             @pl.when((place[d] < Z - 1) & (s <= place[d]))
             def _():
                 for a in (0, 1):
                     for h in (0, 1):
                         line_send(d, a, s, h).wait_send()
-    local(acc, part_o, 1).wait()
+    local(acc, part_o, 6).wait()
 
 
 def line_step(x, dy, pre, w_in, w_down):
@@ -399,11 +431,12 @@
         line_kernel,
         out_shape=[
             sds((R, D), BF16), sds((R, D), BF16), sds((R // 2, F), BF16), sds((F, D), BF16), sds((F, D), F32),
-            sds((H, D), F32), sds((H, D), F32), sds((H, D), BF16), sds((H, D), BF16),
+            sds((EARLY + MID, D), F32), sds((B - EARLY - MID, D), F32),
+            sds((MID, D), BF16), sds((B - EARLY - MID, D), BF16), sds((EARLY + MID, D), BF16),
             sds((2, Z, B, D), BF16), sds((Z, B, D), BF16), sds((Z, B, D), BF16),
         ],
         in_specs=[hbm] * 5,
-        out_specs=[hbm] * 12,
+        out_specs=[hbm] * 13,
         scratch_shapes=[
             pltpu.VMEM((D, F), BF16), pltpu.VMEM((F, D), BF16), pltpu.VMEM((F, D), F32),
             pltpu.VMEM((R, F), BF16), pltpu.VMEM((PAD, D), BF16), pltpu.VMEM((B, F), BF16),
@@ -419,46 +452,69 @@
     )(x, dy, pre, w_in, w_down)
 
 
-def finish_kernel(a_ref, b_ref, part_ref, w_ref, base_ref, came_ref, o_ref, wo_ref, dx_ref):
+def dw_kernel(a_ref, b_ref, part_ref, o_ref):
     rows, width = part_ref.shape[0], b_ref.shape[1]
     for i in (0, 1):
         band = pl.ds(i * rows, rows)
         g = lax.dot_general(a_ref[:, band], b_ref[...], TN, preferred_element_type=F32)
         o_ref[band, :] = (part_ref[:, pl.ds(i * width, width)] + g).astype(o_ref.dtype)
-    wo_ref[...] = w_ref[...]
-
-    @pl.when(pl.program_id(0) == 0)
-    def _():
-        dx_ref[...] = (base_ref[...] + came_ref[...].astype(F32)).astype(dx_ref.dtype)
-
-
-def finish(x, d_pre, part, dw_down, base, came):
+
+
+def finish_dw(x, d_pre, part):
     D = x.shape[1]
     R, F = d_pre.shape
     n = D // (2 * TILE)
-    H = came.shape[0]
+    last = x.shape[0] // R - 1
+    return pl.pallas_call(
+        dw_kernel,
+        grid=(n,),
+        out_shape=jax.ShapeDtypeStruct((D, F), BF16),
+        in_specs=[pl.BlockSpec((R, D // n), lambda i: (last, i)), pl.BlockSpec((R, F), lambda i: (0, 0)),
+                  pl.BlockSpec((F // n, D), lambda i: (i, 0))],
+        out_specs=pl.BlockSpec((D // n, F), lambda i: (i, 0)),
+        compiler_params=pltpu.CompilerParams(vmem_limit_bytes=48 * 1024 * 1024),
+        cost_estimate=pl.CostEstimate(flops=2 * R * D * F, bytes_accessed=2 * (R * D + R * F + 3 * D * F), transcendentals=0),
+    )(x, d_pre, part)
+
+
+def pass_kernel(w_ref, base_ref, came_ref, mid_ref, wo_ref, dx_ref):
+    wo_ref[...] = w_ref[...]
+
+    @pl.when(pl.program_id(0) == 0)
+    def _():
+        for first, count, more in ((0, EARLY, None), (EARLY, MID, mid_ref)):
+            rows = pl.ds(first, count)
+            total = base_ref[rows, :] + came_ref[rows, :].astype(F32)
+            if more is not None:
+                total = total + more[...].astype(F32)
+            dx_ref[rows, :] = total.astype(dx_ref.dtype)
+
+
+def pass_on(dw_down, base, came, mid, rows):
+    F, D = dw_down.shape
     sds = jax.ShapeDtypeStruct
-    first = pl.BlockSpec((H, D), lambda i: (0, 0))
-    band = pl.BlockSpec((F // n, D), lambda i: (i, 0))
+    down = pl.BlockSpec((F // 2, D), lambda i: (i, 0))
+    strip = pl.BlockSpec((EARLY + MID, D), lambda i: (0, 0))
     return pl.pallas_call(
-        finish_kernel,
-        grid=(n,),
-        out_shape=[sds((D, F), BF16), sds((F, D), BF16), sds((2 * H, D), BF16)],
-        in_specs=[pl.BlockSpec((R, D // n), lambda i: (1, i)), pl.BlockSpec((R, F), lambda i: (0, 0)),
-                  band, band, first, first],
-        out_specs=[pl.BlockSpec((D // n, F), lambda i: (i, 0)), band, first],
-        compiler_params=pltpu.CompilerParams(vmem_limit_bytes=56 * 1024 * 1024),
-        cost_estimate=pl.CostEstimate(flops=2 * R * D * F, bytes_accessed=2 * (R * D + R * F + 5 * D * F), transcendentals=0),
-    )(x, d_pre, part, dw_down, base, came)
+        pass_kernel,
+        grid=(2,),
+        out_shape=[sds((F, D), BF16), sds((rows, D), BF16)],
+        in_specs=[down, strip, strip, pl.BlockSpec((MID, D), lambda i: (0, 0))],
+        out_specs=[down, strip],
+        compiler_params=pltpu.CompilerParams(vmem_limit_bytes=32 * 1024 * 1024),
+        cost_estimate=pl.CostEstimate(flops=4 * F * D * 512, bytes_accessed=4 * F * D, transcendentals=0),
+    )(dw_down, base, came, mid)
 
 
 def solution(mesh):
     def body(x, dy, pre, w_in, w_down):
-        xg, _, d_pre, dw_down, part, base, late_base, last, came, _, _, _ = line_step(x, dy, pre, w_in, w_down)
-        hops = [(2 + c, c) for c in (0, 1)] + [(2 * Z - 4 + c, 2 * Z - 2 + c) for c in (0, 1)]
-        late = lax.ppermute(last, "tp", hops)
-        dw_in, dw_down, dx = finish(xg, d_pre, part, dw_down, base, came)
-        dx = lax.dynamic_update_slice(dx, (late_base + late.astype(F32)).astype(BF16), (came.shape[0], 0))
+        xg, _, d_pre, dw_down, part, base, late_base, mid, last, came, _, _, _ = line_step(x, dy, pre, w_in, w_down)
+        hops = [[(2 + c, c), (2 * Z - 4 + c, 2 * Z - 2 + c)] for c in (0, 1)]
+        mid = lax.ppermute(mid, "tp", hops[0])
+        last = lax.ppermute(last, "tp", hops[0] + hops[1])
+        dw_in = finish_dw(xg, d_pre, part)
+        dw_down, dx = pass_on(dw_down, base, came, mid, x.shape[0])
+        dx = lax.dynamic_update_slice(dx, (late_base + last.astype(F32)).astype(BF16), (EARLY + MID, 0))
         return dx, dw_in, dw_down
 
     rows = P(("dp", "tp"), None)

time: 332 us -> 327 us (0.985)
  Pallas kernels: 326 us -> 307 us
  waiting for transfers between devices: 2.23 us -> 13.4 us
    pallas_call x1, Pallas kernels: 303 us -> 286 us  [line_step(): pl.pallas_call(line_kernel, out_shape=[sds((R, D), BF16), sds((R, D), BF1...]
    ppermute x1 -> x2, waiting for transfers between devices: 2.23 us -> 13.4 us  [the longest x1 13.4 us: body(): last = lax.ppermute(last, 'tp', hops[0] + hops[1])]
    pallas_call x1 -> x2, Pallas kernels: 22.9 us -> 20.6 us  [the longest x1 16.9 us: finish_dw(): pl.pallas_call(dw_kernel, grid=(n,), out_shape=jax.ShapeDtypeStruct((D, F...]
  transfers between devices with their start and end apart: 1 -> 2, of which waited for: 1 -> 1; matrix products, arithmetic and copies ran while one was open for 0% -> 0% of each run, Pallas kernels for 7% -> 6%
where the time goes in v3:
time: 327 us
  Pallas kernels  307 us (94%)
  waiting for transfers between devices  13.4 us (4%)
    pallas_call x1, Pallas kernels, line_step(): pl.pallas_call(line_kernel, out_shape=[sds((R, D), BF16), sds((R, D), BF1...  286 us
    pallas_call x1, Pallas kernels, finish_dw(): pl.pallas_call(dw_kernel, grid=(n,), out_shape=jax.ShapeDtypeStruct((D, F...  16.9 us
    ppermute x1, waiting for transfers between devices, body(): last = lax.ppermute(last, 'tp', hops[0] + hops[1])  13.4 us
  transfers between devices with their start and end apart: 2, of which 1 were waited for; matrix products, arithmetic and copies ran while one was open for 0% of the time, Pallas kernels for 6%

profile of v3, /device:TPU:0, one launch (start us, length us, event | category | flops | bytes accessed | tf_op | source)
XLA Modules:
  0.0 326.6 jit_solution(12244367452355554400)
XLA Ops:
  0.6 285.9 %shard_map.76 = (bf16[3328,2560]{1,0:T(8,128)(2,1)}, bf16[3328,2560]{1,0:T(8,128)(2,1)}, bf16[1664,1280]{1,0:T(8,128)(2,1)}, bf16[1280,2560]{1,0:T(8,128)(2,1)},...) custom-call(bf16[416,2560]{1,0:T(8,128)(2,1)} %x_ref.1, ...), custom_call_target="tpu_custom_call" | custom-call | flops 65431142400 | bytes 102236160 | tf_op jit(solution)/shard_map/pallas_call | solution.py:430
  286.6 1.3 collective-permute-start
  287.9 1.3 collective-permute-start.1
  289.2 0.0 copy-start
  289.2 2.2 copy-done
  291.4 0.0 copy-start.1
  291.4 0.0 copy-start.2
  291.4 0.0 copy-start.3
  291.4 16.9 %shard_map.78 = bf16[2560,1280]{1,0:T(8,128)(2,1)} custom-call(bf16[3328,2560]{1,0:T(8,128)(2,1)} %get-tuple-element.21.a_ref, bf16[1664,1280]{1,0:T(8,128)(2,1)S(1)} %copy-done, f32[1280,2560]{1,0:T(8,128)} %get-tuple-element.23.part_ref), custom_call_target="tpu_custom_call" | custom-call | flops 10905190400 | bytes 32440320 | tf_op jit(solution)/shard_map/pallas_call | solution.py:468
  308.3 0.0 collective-permute-done.mid_ref
  308.3 0.0 copy-done.1
  308.4 0.0 copy-done.2
  308.4 0.0 copy-done.3
  308.4 0.0 copy-start.4
  308.4 3.6 %shard_map.77 = (bf16[1280,2560]{1,0:T(8,128)(2,1)}, bf16[416,2560]{1,0:T(8,128)(2,1)}) custom-call(bf16[1280,2560]{1,0:T(8,128)(2,1)S(1)} %copy-done.1, f32[192,2560]{1,0:T(8,128)S(1)} %copy-done.2, bf16[192,2560]{1,0:T(8,128)(2,1)S(1)} %copy-done.3, bf16[160,2560]{1,0:T(8,128)(2,1)S(1)} %collective-permute-done.mid_ref), custom_call_target="tpu_custom_call" | custom-call | flops 6710886400 | bytes 13107200 | tf_op jit(solution)/shard_map/pallas_call | solution.py:498
  312.0 13.4 %collective-permute-done.1 = bf16[224,2560]{1,0:T(8,128)(2,1)S(1)} collective-permute-done((bf16[224,2560]{1,0:T(8,128)(2,1)}, bf16[224,2560]{1,0:T(8,128)(2,1)S(1)}, u32[]{:S(2)}, u32[]{:S(2)}) %collective-permute-start.1) | collective-permute-done | bytes 1146912 | tf_op jit(solution)/shard_map/ppermute | solution.py:514
  325.4 0.0 copy-done.4
  325.4 1.2 fusion
Async XLA Ops:
  286.6 21.8 %collective-permute-start = (bf16[160,2560]{1,0:T(8,128)(2,1)}, bf16[160,2560]{1,0:T(8,128)(2,1)S(1)}, u32[]{:S(2)}, u32[]{:S(2)}) collective-permute-start(bf16[160,2560]{1,0:T(8,128)(2,1)} %get-tuple-element.17), channel_id=1, source_target_pairs={{2,0},{4,6},{10,8},{12,14},{18,16},{20,22},{26,24},{28,30}} | collective-permute-start | bytes 2457608 | tf_op jit(solution)/shard_map/ppermute | solution.py:513
  287.9 37.5 %collective-permute-start.1 = (bf16[224,2560]{1,0:T(8,128)(2,1)}, bf16[224,2560]{1,0:T(8,128)(2,1)S(1)}, u32[]{:S(2)}, u32[]{:S(2)}) collective-permute-start(bf16[224,2560]{1,0:T(8,128)(2,1)} %get-tuple-element.20), channel_id=1, source_target_pairs={{2,0},{4,6},{3,1},{5,7},{10,8},{12,14},{11,9},{13,15},{18,16},{20,... | collective-permute-start | bytes 3440648 | tf_op jit(solution)/shard_map/ppermute | solution.py:514
  289.2 2.2 copy-start
  291.4 17.0 %copy-start.1 = (bf16[1280,2560]{1,0:T(8,128)(2,1)S(1)}, bf16[1280,2560]{1,0:T(8,128)(2,1)}, u32[]{:S(2)}) copy-start(bf16[1280,2560]{1,0:T(8,128)(2,1)} %get-tuple-element.14.w_ref) | copy-start | bytes 19660804
  291.4 17.0 %copy-start.2 = (f32[192,2560]{1,0:T(8,128)S(1)}, f32[192,2560]{1,0:T(8,128)}, u32[]{:S(2)}) copy-start(f32[192,2560]{1,0:T(8,128)} %get-tuple-element.15.base_ref) | copy-start | bytes 5898244
  291.4 17.0 %copy-start.3 = (bf16[192,2560]{1,0:T(8,128)(2,1)S(1)}, bf16[192,2560]{1,0:T(8,128)(2,1)}, u32[]{:S(2)}) copy-start(bf16[192,2560]{1,0:T(8,128)(2,1)} %get-tuple-element.16.came_ref) | copy-start | bytes 2949124
  308.4 17.0 %copy-start.4 = (f32[224,2560]{1,0:T(8,128)S(1)}, f32[224,2560]{1,0:T(8,128)}, u32[]{:S(2)}) copy-start(f32[224,2560]{1,0:T(8,128)} %get-tuple-element.19) | copy-start | bytes 6881284

commit v4 on v3

--- a/solution.py
+++ b/solution.py
@@ -14,7 +14,7 @@
 K0 = 0.7978845608028654
 K1 = 0.044715
 TILE = 256
-EARLY, MID = 32, 160
+EARLY, MID = 64, 128
 
 
 def gelu_and_slope(p):
@@ -27,9 +27,9 @@
 
 def line_kernel(
     x_ref, dy_ref, pre_ref, wi_ref, wd_ref,
-    xg, dyg, dpre_o, dwd_o, part_o, base_o, late_base_o, mid_o, last_o, came_o, rin, pin, rout,
+    xg, dyg, dpre_o, dwd_o, part_o, base_o, last_base_o, mid_o, last_o, came_o, rin, pin, rout,
     wi, wd, acc, dp, dyb, preb, hid, pxb, pv, rv, sb, bb,
-    ssem, rsem, ps, pr, pxs, pxr, rs_s, rs_r, lsem,
+    ssem, rsem, ps, pr, pxs, pxr, rs_s, rs_r, lsem, in_sem,
 ):
     B, D = dy_ref.shape
     H = B // 2
@@ -71,6 +71,9 @@
         outer = (zz == 0) | (zz == Z - 1)
         return jnp.where(outer, p, jnp.where(p < 2, 1 - p, p))
 
+    def settle():
+        sync(pre_ref.at[pl.ds(0, 16)], preb.at[pl.ds(0, 16)], 5)
+
     def rows_of(chip, core, h):
         return pl.ds(pl.multiple_of((chip * 2 + core) * B + h * H, 16), H)
 
@@ -83,13 +86,20 @@
     def half(h):
         return pl.ds(pl.multiple_of(h * H, 16), H)
 
+    def signal(sem, to):
+        pl.semaphore_signal(sem, inc=1, device_id={"tp": to}, device_id_type=pl.DeviceIdType.MESH)
+
     barrier = pltpu.get_barrier_semaphore()
-    pl.semaphore_signal(barrier, inc=1, device_id={"tp": partner}, device_id_type=pl.DeviceIdType.MESH)
+    signal(barrier, partner)
     for d in (0, 1):
-        @pl.when(place[d] < Z - 1)
-        def _():
-            pl.semaphore_signal(barrier, inc=1, device_id={"tp": ahead[d]}, device_id_type=pl.DeviceIdType.MESH)
-    pl.semaphore_wait(barrier, jnp.where((z > 0) & (z < Z - 1), 3, 2))
+        @pl.when((place[d] < Z - 1) & ((d == 0) | (z != 2)))
+        def _():
+            signal(barrier, ahead[d])
+    pl.semaphore_wait(barrier, jnp.where(z == 2, 3, 2))
+
+    @pl.when(z == 2)
+    def _():
+        signal(in_sem, ahead[1])
 
     def own_send(d, a, h):
         return remote(arrs[a].at[half(h)], gathered[a].at[rows_of(spot(a, z + sign[d], z), c, h)],
@@ -120,10 +130,14 @@
         return remote(gathered[a].at[r], gathered[a].at[r],
                       ps.at[a, chip, h], pr.at[a, chip, h], partner)
 
-    for h in (0, 1):
-        for d in (0, 1):
-            @pl.when(place[d] < Z - 1)
-            def _():
+    for d in (1, 0):
+        @pl.when(place[d] < Z - 1)
+        def _():
+            if d == 0:
+                @pl.when(z == 1)
+                def _():
+                    pl.semaphore_wait(in_sem, 1)
+            for h in (0, 1):
                 own_send(d, 0, h).start()
     for h in (0, 1):
         own_to_partner(0, h).start()
@@ -183,6 +197,7 @@
 
         @pl.when(t == 12)
         def _():
+            settle()
             local(acc, part_o, 6).start()
 
         def rs(j, _):
@@ -202,7 +217,15 @@
                 @pl.when(hh == 0)
                 def _():
                     remote(pxb, pin.at[b], pxs.at[0], pxr.at[b], partner).wait_recv()
-                local(pin.at[b, half(hh)], pv, 0).start()
+                sync(pin.at[b, half(hh)], pv, 0)
+
+                def own(n, _):
+                    cs = cols(n)
+                    g = lax.dot_general(dp[rows_of(b, c, hh), :], wi[cs, :], NT, preferred_element_type=F32)
+                    bb[:, cs] = g + pv[:, cs].astype(F32)
+                    return 0
+
+                lax.fori_loop(0, D // TILE, own, 0)
                 for d in (0, 1):
                     @pl.when(has[d])
                     def _():
@@ -213,7 +236,6 @@
                     @pl.when(jnp.logical_not(has[d]))
                     def _():
                         rv[d] = jnp.zeros(rv.shape[1:], BF16)
-                local(pin.at[b, half(hh)], pv, 0).wait()
                 for d in (0, 1):
                     @pl.when(has[d])
                     def _():
@@ -221,9 +243,7 @@
 
                 def tile(n, _):
                     cs = cols(n)
-                    g = lax.dot_general(dp[rows_of(b, c, hh), :], wi[cs, :], NT, preferred_element_type=F32)
-                    g = g + pv[:, cs].astype(F32)
-                    g = g + (rv[0, :, cs].astype(F32) + rv[1, :, cs].astype(F32))
+                    g = bb[:, cs] + (rv[0, :, cs].astype(F32) + rv[1, :, cs].astype(F32))
                     bb[:, cs] = g
                     sb[:, cs] = g.astype(BF16)
                     return 0
@@ -235,11 +255,11 @@
                     @pl.when(hh == 0)
                     def _():
                         sync(bb.at[pl.ds(0, early + mid)], base_o, 3)
-                        sync(bb.at[pl.ds(early + mid, rest)], late_base_o.at[pl.ds(0, rest)], 3)
+                        sync(bb.at[pl.ds(early + mid, rest)], last_base_o.at[pl.ds(0, rest)], 3)
 
                     @pl.when(hh == 1)
                     def _():
-                        sync(bb, late_base_o.at[pl.ds(rest, H)], 3)
+                        sync(bb, last_base_o.at[pl.ds(rest, H)], 3)
 
                 @pl.when(to_end)
                 def _():
@@ -322,6 +342,7 @@
                     return 0
 
                 lax.fori_loop(0, D // TILE, px, 0)
+                settle()
                 px_send(chip, k).start()
 
             def t2(m, _):
@@ -331,11 +352,8 @@
 
             lax.fori_loop(0, F // TILE, t2, 0)
 
-        @pl.when(t == 8)
-        def _():
-            for k in (2, 3):
-                local(dp.at[chip_rows(turn(z, k))], dpre_o.at[pl.ds((k - 2) * 2 * B, 2 * B)], 2 + k).start()
-
+        @pl.when(t == 2)
+        def _():
             pv[...] = jnp.zeros(pv.shape, BF16)
 
             @pl.when(((z > 0) & (z < Z - 1)) | (c == 0))
@@ -347,6 +365,11 @@
                 sync(pv.at[pl.ds(0, early)], came_o.at[pl.ds(0, early)], 1)
             sync(x_ref, dyb.at[pl.ds(0, B)], 1)
             sync(dyb.at[pl.ds(0, B)], xg.at[block_of(spot(1, z, z), c)], 1)
+
+        @pl.when(t == 8)
+        def _():
+            for k in (2, 3):
+                local(dp.at[chip_rows(turn(z, k))], dpre_o.at[pl.ds((k - 2) * 2 * B, 2 * B)], 2 + k).start()
 
             def flush(m, _):
                 ms = cols(m)
@@ -443,7 +466,7 @@
             pltpu.VMEM((PAD, F), BF16), pltpu.VMEM((B, D), BF16), pltpu.VMEM((H, D), BF16),
             pltpu.VMEM((2, H, D), BF16), pltpu.VMEM((H, D), BF16), pltpu.VMEM((H, D), F32),
             dma((2, 2, 3, 2)), dma((2, 2, 3, 2)), dma((2, Z, 2)), dma((2, Z, 2)),
-            dma((Z,)), dma((Z,)), dma((Z, 2)), dma((2, Z, 2)), dma((8,)),
+            dma((Z,)), dma((Z,)), dma((Z, 2)), dma((2, Z, 2)), dma((8,)), pltpu.SemaphoreType.REGULAR,
         ],
         compiler_params=pltpu.CompilerParams(
             collective_id=0, has_side_effects=True, vmem_limit_bytes=62 * 1024 * 1024
@@ -508,13 +531,13 @@
 
 def solution(mesh):
     def body(x, dy, pre, w_in, w_down):
-        xg, _, d_pre, dw_down, part, base, late_base, mid, last, came, _, _, _ = line_step(x, dy, pre, w_in, w_down)
+        xg, _, d_pre, dw_down, part, base, last_base, mid, last, came, _, _, _ = line_step(x, dy, pre, w_in, w_down)
         hops = [[(2 + c, c), (2 * Z - 4 + c, 2 * Z - 2 + c)] for c in (0, 1)]
         mid = lax.ppermute(mid, "tp", hops[0])
         last = lax.ppermute(last, "tp", hops[0] + hops[1])
         dw_in = finish_dw(xg, d_pre, part)
         dw_down, dx = pass_on(dw_down, base, came, mid, x.shape[0])
-        dx = lax.dynamic_update_slice(dx, (late_base + last.astype(F32)).astype(BF16), (EARLY + MID, 0))
+        dx = lax.dynamic_update_slice(dx, (last_base + last.astype(F32)).astype(BF16), (EARLY + MID, 0))
         return dx, dw_in, dw_down
 
     rows = P(("dp", "tp"), None)

time: 327 us -> 327 us (level)
  no operation moved by 1% of the time
where the time goes in v4:
time: 327 us; the launch traced here: 326 us
  Pallas kernels  307 us (94%)
  waiting for transfers between devices  11.9 us (4%)
    pallas_call x1, Pallas kernels, line_step(): pl.pallas_call(line_kernel, out_shape=[sds((R, D), BF16), sds((R, D), BF1...  287 us
    pallas_call x1, Pallas kernels, finish_dw(): pl.pallas_call(dw_kernel, grid=(n,), out_shape=jax.ShapeDtypeStruct((D, F...  16.9 us
    ppermute x1, waiting for transfers between devices, body(): last = lax.ppermute(last, 'tp', hops[0] + hops[1])  11.9 us
  transfers between devices with their start and end apart: 2, of which 1 were waited for; matrix products, arithmetic and copies ran while one was open for 0% of the time, Pallas kernels for 6%

profile of v4, /device:TPU:0, one launch (start us, length us, event | category | flops | bytes accessed | tf_op | source)
XLA Modules:
  0.0 325.9 jit_solution(18156299774123122078)
XLA Ops:
  0.6 286.7 %shard_map.76 = (bf16[3328,2560]{1,0:T(8,128)(2,1)}, bf16[3328,2560]{1,0:T(8,128)(2,1)}, bf16[1664,1280]{1,0:T(8,128)(2,1)}, bf16[1280,2560]{1,0:T(8,128)(2,1)},...) custom-call(bf16[416,2560]{1,0:T(8,128)(2,1)} %x_ref.1, ...), custom_call_target="tpu_custom_call" | custom-call | flops 65431142400 | bytes 102236160 | tf_op jit(solution)/shard_map/pallas_call | solution.py:453
  287.3 1.3 collective-permute-start
  288.6 1.3 collective-permute-start.1
  289.9 0.0 copy-start
  289.9 2.2 copy-done
  292.1 0.0 copy-start.1
  292.1 0.0 copy-start.2
  292.1 0.0 copy-start.3
  292.1 16.9 %shard_map.78 = bf16[2560,1280]{1,0:T(8,128)(2,1)} custom-call(bf16[3328,2560]{1,0:T(8,128)(2,1)} %get-tuple-element.21.a_ref, bf16[1664,1280]{1,0:T(8,128)(2,1)S(1)} %copy-done, f32[1280,2560]{1,0:T(8,128)} %get-tuple-element.23.part_ref), custom_call_target="tpu_custom_call" | custom-call | flops 10905190400 | bytes 32440320 | tf_op jit(solution)/shard_map/pallas_call | solution.py:491
  309.1 0.0 collective-permute-done.mid_ref
  309.1 0.0 copy-done.1
  309.1 0.0 copy-done.2
  309.1 0.0 copy-done.3
  309.1 0.0 copy-start.4
  309.1 3.6 %shard_map.77 = (bf16[1280,2560]{1,0:T(8,128)(2,1)}, bf16[416,2560]{1,0:T(8,128)(2,1)}) custom-call(bf16[1280,2560]{1,0:T(8,128)(2,1)S(1)} %copy-done.1, f32[192,2560]{1,0:T(8,128)S(1)} %copy-done.2, bf16[192,2560]{1,0:T(8,128)(2,1)S(1)} %copy-done.3, bf16[128,2560]{1,0:T(8,128)(2,1)S(1)} %collective-permute-done.mid_ref), custom_call_target="tpu_custom_call" | custom-call | flops 6710886400 | bytes 13107200 | tf_op jit(solution)/shard_map/pallas_call | solution.py:521
  312.7 11.9 %collective-permute-done.1 = bf16[224,2560]{1,0:T(8,128)(2,1)S(1)} collective-permute-done((bf16[224,2560]{1,0:T(8,128)(2,1)}, bf16[224,2560]{1,0:T(8,128)(2,1)S(1)}, u32[]{:S(2)}, u32[]{:S(2)}) %collective-permute-start.1) | collective-permute-done | bytes 1146912 | tf_op jit(solution)/shard_map/ppermute | solution.py:537
  324.6 0.0 copy-done.4
  324.6 1.2 fusion
Async XLA Ops:
  287.3 21.8 %collective-permute-start = (bf16[128,2560]{1,0:T(8,128)(2,1)}, bf16[128,2560]{1,0:T(8,128)(2,1)S(1)}, u32[]{:S(2)}, u32[]{:S(2)}) collective-permute-start(bf16[128,2560]{1,0:T(8,128)(2,1)} %get-tuple-element.17), channel_id=1, source_target_pairs={{2,0},{4,6},{10,8},{12,14},{18,16},{20,22},{26,24},{28,30}} | collective-permute-start | bytes 1966088 | tf_op jit(solution)/shard_map/ppermute | solution.py:536
  288.6 36.0 %collective-permute-start.1 = (bf16[224,2560]{1,0:T(8,128)(2,1)}, bf16[224,2560]{1,0:T(8,128)(2,1)S(1)}, u32[]{:S(2)}, u32[]{:S(2)}) collective-permute-start(bf16[224,2560]{1,0:T(8,128)(2,1)} %get-tuple-element.20), channel_id=1, source_target_pairs={{2,0},{4,6},{3,1},{5,7},{10,8},{12,14},{11,9},{13,15},{18,16},{20,... | collective-permute-start | bytes 3440648 | tf_op jit(solution)/shard_map/ppermute | solution.py:537
  289.9 2.2 copy-start
  292.1 17.0 %copy-start.1 = (bf16[1280,2560]{1,0:T(8,128)(2,1)S(1)}, bf16[1280,2560]{1,0:T(8,128)(2,1)}, u32[]{:S(2)}) copy-start(bf16[1280,2560]{1,0:T(8,128)(2,1)} %get-tuple-element.14.w_ref) | copy-start | bytes 19660804
  292.1 17.0 %copy-start.2 = (f32[192,2560]{1,0:T(8,128)S(1)}, f32[192,2560]{1,0:T(8,128)}, u32[]{:S(2)}) copy-start(f32[192,2560]{1,0:T(8,128)} %get-tuple-element.15.base_ref) | copy-start | bytes 5898244
  292.1 17.0 %copy-start.3 = (bf16[192,2560]{1,0:T(8,128)(2,1)S(1)}, bf16[192,2560]{1,0:T(8,128)(2,1)}, u32[]{:S(2)}) copy-start(bf16[192,2560]{1,0:T(8,128)(2,1)} %get-tuple-element.16.came_ref) | copy-start | bytes 2949124
  309.1 15.5 %copy-start.4 = (f32[224,2560]{1,0:T(8,128)S(1)}, f32[224,2560]{1,0:T(8,128)}, u32[]{:S(2)}) copy-start(f32[224,2560]{1,0:T(8,128)} %get-tuple-element.19) | copy-start | bytes 6881284

commit v5 on v4

--- a/solution.py
+++ b/solution.py
@@ -72,7 +72,7 @@
         return jnp.where(outer, p, jnp.where(p < 2, 1 - p, p))
 
     def settle():
-        sync(pre_ref.at[pl.ds(0, 16)], preb.at[pl.ds(0, 16)], 5)
+        sync(hid.at[pl.ds(0, 16), :], rout.at[z, pl.ds(0, 16), pl.ds(0, F)], 8)
 
     def rows_of(chip, core, h):
         return pl.ds(pl.multiple_of((chip * 2 + core) * B + h * H, 16), H)
@@ -141,8 +141,11 @@
                 own_send(d, 0, h).start()
     for h in (0, 1):
         own_to_partner(0, h).start()
-    local(wd_ref, wd, 6).start()
-    local(wi_ref, wi, 7).start()
+    local(dy_ref, dyb.at[pl.ds(0, B)], 1).start()
+    local(pre_ref.at[block_of(z, c)], preb, 0).start()
+    local(wd_ref, wd, 10).start()
+    local(wi_ref, wi, 11).start()
+    local(x_ref, pxb, 12).start()
     for h in (0, 1):
         own_to_partner(1, h).start()
 
@@ -154,8 +157,8 @@
         return 0
 
     lax.fori_loop(0, F // 64, zero, 0)
-    local(wd_ref, wd, 6).wait()
-    local(wi_ref, wi, 7).wait()
+    local(wd_ref, wd, 10).wait()
+    local(wi_ref, wi, 11).wait()
 
     def arrive(d, a, s, h):
         line_arrival(d, a, s, h).wait_recv()
@@ -198,7 +201,25 @@
         @pl.when(t == 12)
         def _():
             settle()
-            local(acc, part_o, 6).start()
+            local(acc, part_o, 9).start()
+
+        def start_load(a, k):
+            core = jnp.where(t % 2 == 0, c, 1 - c)
+            chip = turn(z, k)
+
+            @pl.when(t % 2 == 1)
+            def _():
+                for hh in (0, 1):
+                    from_partner(a, chip, hh).wait_recv()
+            local(gathered[a].at[block_of(spot(a, z, chip), core)], dyb.at[pl.ds(0, B)], 1).start()
+
+        @pl.when((t > 0) & (t < 8))
+        def _():
+            start_load(0, t // 2)
+
+        @pl.when((t >= 8) & (t < 12))
+        def _():
+            start_load(1, (t - 8) // 2)
 
         def rs(j, _):
             outer = (z == 0) | (z == Z - 1)
@@ -217,33 +238,35 @@
                 @pl.when(hh == 0)
                 def _():
                     remote(pxb, pin.at[b], pxs.at[0], pxr.at[b], partner).wait_recv()
-                sync(pin.at[b, half(hh)], pv, 0)
+                local(pin.at[b, half(hh)], pv, 4).start()
+                for d in (0, 1):
+                    @pl.when(has[d])
+                    def _():
+                        remote(rin.at[d, b, half(hh)], rin.at[d, b, half(hh)],
+                               rs_s.at[b, hh], rs_r.at[d, b, hh], partner).wait_recv()
+                        local(rin.at[d, b, half(hh)], rv.at[d], 5 + d).start()
+
+                    @pl.when(jnp.logical_not(has[d]))
+                    def _():
+                        rv[d] = jnp.zeros(rv.shape[1:], BF16)
 
                 def own(n, _):
                     cs = cols(n)
-                    g = lax.dot_general(dp[rows_of(b, c, hh), :], wi[cs, :], NT, preferred_element_type=F32)
-                    bb[:, cs] = g + pv[:, cs].astype(F32)
+                    bb[:, cs] = lax.dot_general(
+                        dp[rows_of(b, c, hh), :], wi[cs, :], NT, preferred_element_type=F32)
                     return 0
 
                 lax.fori_loop(0, D // TILE, own, 0)
+                local(pin.at[b, half(hh)], pv, 4).wait()
                 for d in (0, 1):
                     @pl.when(has[d])
                     def _():
-                        remote(rin.at[d, b, half(hh)], rin.at[d, b, half(hh)],
-                               rs_s.at[b, hh], rs_r.at[d, b, hh], partner).wait_recv()
-                        local(rin.at[d, b, half(hh)], rv.at[d], 1 + d).start()
-
-                    @pl.when(jnp.logical_not(has[d]))
-                    def _():
-                        rv[d] = jnp.zeros(rv.shape[1:], BF16)
-                for d in (0, 1):
-                    @pl.when(has[d])
-                    def _():
-                        local(rin.at[d, b, half(hh)], rv.at[d], 1 + d).wait()
+                        local(rin.at[d, b, half(hh)], rv.at[d], 5 + d).wait()
 
                 def tile(n, _):
                     cs = cols(n)
-                    g = bb[:, cs] + (rv[0, :, cs].astype(F32) + rv[1, :, cs].astype(F32))
+                    g = bb[:, cs] + pv[:, cs].astype(F32)
+                    g = g + (rv[0, :, cs].astype(F32) + rv[1, :, cs].astype(F32))
                     bb[:, cs] = g
                     sb[:, cs] = g.astype(BF16)
                     return 0
@@ -254,19 +277,19 @@
                 def _():
                     @pl.when(hh == 0)
                     def _():
-                        sync(bb.at[pl.ds(0, early + mid)], base_o, 3)
-                        sync(bb.at[pl.ds(early + mid, rest)], last_base_o.at[pl.ds(0, rest)], 3)
+                        sync(bb.at[pl.ds(0, early + mid)], base_o, 7)
+                        sync(bb.at[pl.ds(early + mid, rest)], last_base_o.at[pl.ds(0, rest)], 7)
 
                     @pl.when(hh == 1)
                     def _():
-                        sync(bb, last_base_o.at[pl.ds(rest, H)], 3)
+                        sync(bb, last_base_o.at[pl.ds(rest, H)], 7)
 
                 @pl.when(to_end)
                 def _():
                     @pl.when(hh == 0)
                     def _():
-                        sync(sb.at[pl.ds(0, early)], rout.at[b, pl.ds(0, early)], 3)
-                        sync(sb.at[pl.ds(early, mid)], mid_o, 3)
+                        sync(sb.at[pl.ds(0, early)], rout.at[b, pl.ds(0, early)], 7)
+                        sync(sb.at[pl.ds(early, mid)], mid_o, 7)
                         for d in (0, 1):
                             @pl.when((b > z) if d == 0 else (b < z))
                             def _():
@@ -275,15 +298,15 @@
                                 @pl.when(c == 1)
                                 def _():
                                     mid_send(d, b).start()
-                        sync(sb.at[pl.ds(early + mid, rest)], last_o.at[pl.ds(0, rest)], 3)
+                        sync(sb.at[pl.ds(early + mid, rest)], last_o.at[pl.ds(0, rest)], 7)
 
                     @pl.when(hh == 1)
                     def _():
-                        sync(sb, last_o.at[pl.ds(rest, H)], 3)
+                        sync(sb, last_o.at[pl.ds(rest, H)], 7)
 
                 @pl.when((b != z) & jnp.logical_not(to_end))
                 def _():
-                    sync(sb, rout.at[b, half(hh)], 3)
+                    sync(sb, rout.at[b, half(hh)], 7)
                     for d in (0, 1):
                         @pl.when((b > z) if d == 0 else (b < z))
                         def _():
@@ -303,21 +326,8 @@
             odd = t % 2
             core = jnp.where(odd == 0, c, 1 - c)
             blk = block_of(chip, core)
-            local(pre_ref.at[blk], preb, 0).start()
-
-            @pl.when(odd == 1)
-            def _():
-                for hh in (0, 1):
-                    from_partner(0, chip, hh).wait_recv()
-
-            @pl.when(t == 0)
-            def _():
-                sync(dy_ref, dyb.at[pl.ds(0, B)], 1)
-
-            @pl.when(t > 0)
-            def _():
-                sync(dyg.at[blk], dyb.at[pl.ds(0, B)], 1)
             local(pre_ref.at[blk], preb, 0).wait()
+            local(dy_ref, dyb.at[pl.ds(0, B)], 1).wait()
 
             def t1(n, _):
                 cs = cols(n)
@@ -329,8 +339,22 @@
 
             lax.fori_loop(0, F // TILE, t1, 0)
 
+            @pl.when(t < 7)
+            def _():
+                core = jnp.where(odd == 1, c, 1 - c)
+                local(pre_ref.at[block_of(turn(z, (t + 1) // 2), core)], preb, 0).start()
+
+            @pl.when(t == 0)
+            def _():
+                local(x_ref, pxb, 12).wait()
+                local(pxb, xg.at[block_of(spot(1, z, z), c)], 12).start()
+
             @pl.when(odd == 1)
             def _():
+                @pl.when(k == 0)
+                def _():
+                    local(pxb, xg.at[block_of(spot(1, z, z), c)], 12).wait()
+
                 @pl.when(k > 0)
                 def _():
                     px_send(chip, k - 1).wait_send()
@@ -358,24 +382,23 @@
 
             @pl.when(((z > 0) & (z < Z - 1)) | (c == 0))
             def _():
-                sync(pv.at[pl.ds(0, mid)], came_o.at[pl.ds(early, mid)], 1)
+                sync(pv.at[pl.ds(0, mid)], came_o.at[pl.ds(early, mid)], 13)
 
             @pl.when((z > 0) & (z < Z - 1))
             def _():
-                sync(pv.at[pl.ds(0, early)], came_o.at[pl.ds(0, early)], 1)
-            sync(x_ref, dyb.at[pl.ds(0, B)], 1)
-            sync(dyb.at[pl.ds(0, B)], xg.at[block_of(spot(1, z, z), c)], 1)
+                sync(pv.at[pl.ds(0, early)], came_o.at[pl.ds(0, early)], 13)
 
         @pl.when(t == 8)
         def _():
             for k in (2, 3):
-                local(dp.at[chip_rows(turn(z, k))], dpre_o.at[pl.ds((k - 2) * 2 * B, 2 * B)], 2 + k).start()
+                local(dp.at[chip_rows(turn(z, k))], dpre_o.at[pl.ds((k - 2) * 2 * B, 2 * B)], k).start()
+            px_send(0, 3).wait_send()
 
             def flush(m, _):
                 ms = cols(m)
-                dyb[pl.ds(0, TILE), :] = acc[ms, :].astype(BF16)
+                pxb[pl.ds(0, TILE), :] = acc[ms, :].astype(BF16)
                 acc[ms, :] = jnp.zeros((TILE, D), F32)
-                sync(dyb.at[pl.ds(0, TILE)], dwd_o.at[ms], 1)
+                sync(pxb.at[pl.ds(0, TILE)], dwd_o.at[ms], 13)
                 return 0
 
             lax.fori_loop(0, F // TILE, flush, 0)
@@ -383,15 +406,9 @@
         @pl.when((t >= 8) & (t < 12))
         def _():
             k = (t - 8) // 2
-            odd = t % 2
             chip = turn(z, k)
-            core = jnp.where(odd == 0, c, 1 - c)
-
-            @pl.when(odd == 1)
-            def _():
-                for hh in (0, 1):
-                    from_partner(1, chip, hh).wait_recv()
-            sync(xg.at[block_of(k, core)], dyb.at[pl.ds(0, B)], 1)
+            core = jnp.where(t % 2 == 0, c, 1 - c)
+            local(x_ref, dyb.at[pl.ds(0, B)], 1).wait()
 
             def t4(m, _):
                 for i in (0, 1):
@@ -406,10 +423,9 @@
     lax.fori_loop(0, 13, slot, 0)
 
     for k in (2, 3):
-        local(dp.at[pl.ds(0, 2 * B)], dpre_o.at[pl.ds(0, 2 * B)], 2 + k).wait()
+        local(dp.at[pl.ds(0, 2 * B)], dpre_o.at[pl.ds(0, 2 * B)], k).wait()
         for h in (0, 1):
             from_partner(1, turn(z, k), h).wait_recv()
-    px_send(0, 3).wait_send()
     for chip in range(Z):
         for h in (0, 1):
             for a in (0, 1):
@@ -439,7 +455,7 @@
                 for a in (0, 1):
                     for h in (0, 1):
                         line_send(d, a, s, h).wait_send()
-    local(acc, part_o, 6).wait()
+    local(acc, part_o, 9).wait()
 
 
 def line_step(x, dy, pre, w_in, w_down):
@@ -466,7 +482,7 @@
             pltpu.VMEM((PAD, F), BF16), pltpu.VMEM((B, D), BF16), pltpu.VMEM((H, D), BF16),
             pltpu.VMEM((2, H, D), BF16), pltpu.VMEM((H, D), BF16), pltpu.VMEM((H, D), F32),
             dma((2, 2, 3, 2)), dma((2, 2, 3, 2)), dma((2, Z, 2)), dma((2, Z, 2)),
-            dma((Z,)), dma((Z,)), dma((Z, 2)), dma((2, Z, 2)), dma((8,)), pltpu.SemaphoreType.REGULAR,
+            dma((Z,)), dma((Z,)), dma((Z, 2)), dma((2, Z, 2)), dma((14,)), pltpu.SemaphoreType.REGULAR,
         ],
         compiler_params=pltpu.CompilerParams(
             collective_id=0, has_side_effects=True, vmem_limit_bytes=62 * 1024 * 1024

time: 327 us -> 326 us (level)
  no operation moved by 1% of the time
where the time goes in v5:
time: 326 us
  Pallas kernels  307 us (94%)
  waiting for transfers between devices  11.9 us (4%)
    pallas_call x1, Pallas kernels, line_step(): pl.pallas_call(line_kernel, out_shape=[sds((R, D), BF16), sds((R, D), BF1...  287 us
    pallas_call x1, Pallas kernels, finish_dw(): pl.pallas_call(dw_kernel, grid=(n,), out_shape=jax.ShapeDtypeStruct((D, F...  16.9 us
    ppermute x1, waiting for transfers between devices, body(): last = lax.ppermute(last, 'tp', hops[0] + hops[1])  11.9 us
  transfers between devices with their start and end apart: 2, of which 1 were waited for; matrix products, arithmetic and copies ran while one was open for 0% of the time, Pallas kernels for 6%

profile of v5, /device:TPU:0, one launch (start us, length us, event | category | flops | bytes accessed | tf_op | source)
XLA Modules:
  0.0 325.9 jit_solution(18104513030496399764)
XLA Ops:
  0.6 286.7 %shard_map.76 = (bf16[3328,2560]{1,0:T(8,128)(2,1)}, bf16[3328,2560]{1,0:T(8,128)(2,1)}, bf16[1664,1280]{1,0:T(8,128)(2,1)}, bf16[1280,2560]{1,0:T(8,128)(2,1)},...) custom-call(bf16[416,2560]{1,0:T(8,128)(2,1)} %x_ref.1, ...), custom_call_target="tpu_custom_call" | custom-call | flops 65431142400 | bytes 102236160 | tf_op jit(solution)/shard_map/pallas_call | solution.py:469
  287.4 1.3 collective-permute-start
  288.7 1.3 collective-permute-start.1
  290.0 0.0 copy-start
  290.0 2.2 copy-done
  292.2 0.0 copy-start.1
  292.2 0.0 copy-start.2
  292.2 0.0 copy-start.3
  292.2 16.9 %shard_map.78 = bf16[2560,1280]{1,0:T(8,128)(2,1)} custom-call(bf16[3328,2560]{1,0:T(8,128)(2,1)} %get-tuple-element.21.a_ref, bf16[1664,1280]{1,0:T(8,128)(2,1)S(1)} %copy-done, f32[1280,2560]{1,0:T(8,128)} %get-tuple-element.23.part_ref), custom_call_target="tpu_custom_call" | custom-call | flops 10905190400 | bytes 32440320 | tf_op jit(solution)/shard_map/pallas_call | solution.py:507
  309.1 0.0 collective-permute-done.mid_ref
  309.1 0.0 copy-done.1
  309.1 0.0 copy-done.2
  309.2 0.0 copy-done.3
  309.2 0.0 copy-start.4
  309.2 3.6 %shard_map.77 = (bf16[1280,2560]{1,0:T(8,128)(2,1)}, bf16[416,2560]{1,0:T(8,128)(2,1)}) custom-call(bf16[1280,2560]{1,0:T(8,128)(2,1)S(1)} %copy-done.1, f32[192,2560]{1,0:T(8,128)S(1)} %copy-done.2, bf16[192,2560]{1,0:T(8,128)(2,1)S(1)} %copy-done.3, bf16[128,2560]{1,0:T(8,128)(2,1)S(1)} %collective-permute-done.mid_ref), custom_call_target="tpu_custom_call" | custom-call | flops 6710886400 | bytes 13107200 | tf_op jit(solution)/shard_map/pallas_call | solution.py:537
  312.8 11.9 %collective-permute-done.1 = bf16[224,2560]{1,0:T(8,128)(2,1)S(1)} collective-permute-done((bf16[224,2560]{1,0:T(8,128)(2,1)}, bf16[224,2560]{1,0:T(8,128)(2,1)S(1)}, u32[]{:S(2)}, u32[]{:S(2)}) %collective-permute-start.1) | collective-permute-done | bytes 1146912 | tf_op jit(solution)/shard_map/ppermute | solution.py:553
  324.6 0.0 copy-done.4
  324.6 1.2 fusion
Async XLA Ops:
  287.4 21.8 %collective-permute-start = (bf16[128,2560]{1,0:T(8,128)(2,1)}, bf16[128,2560]{1,0:T(8,128)(2,1)S(1)}, u32[]{:S(2)}, u32[]{:S(2)}) collective-permute-start(bf16[128,2560]{1,0:T(8,128)(2,1)} %get-tuple-element.17), channel_id=1, source_target_pairs={{2,0},{4,6},{10,8},{12,14},{18,16},{20,22},{26,24},{28,30}} | collective-permute-start | bytes 1966088 | tf_op jit(solution)/shard_map/ppermute | solution.py:552
  288.7 36.0 %collective-permute-start.1 = (bf16[224,2560]{1,0:T(8,128)(2,1)}, bf16[224,2560]{1,0:T(8,128)(2,1)S(1)}, u32[]{:S(2)}, u32[]{:S(2)}) collective-permute-start(bf16[224,2560]{1,0:T(8,128)(2,1)} %get-tuple-element.20), channel_id=1, source_target_pairs={{2,0},{4,6},{3,1},{5,7},{10,8},{12,14},{11,9},{13,15},{18,16},{20,... | collective-permute-start | bytes 3440648 | tf_op jit(solution)/shard_map/ppermute | solution.py:553
  290.0 2.2 copy-start
  292.2 17.0 %copy-start.1 = (bf16[1280,2560]{1,0:T(8,128)(2,1)S(1)}, bf16[1280,2560]{1,0:T(8,128)(2,1)}, u32[]{:S(2)}) copy-start(bf16[1280,2560]{1,0:T(8,128)(2,1)} %get-tuple-element.14.w_ref) | copy-start | bytes 19660804
  292.2 17.0 %copy-start.2 = (f32[192,2560]{1,0:T(8,128)S(1)}, f32[192,2560]{1,0:T(8,128)}, u32[]{:S(2)}) copy-start(f32[192,2560]{1,0:T(8,128)} %get-tuple-element.15.base_ref) | copy-start | bytes 5898244
  292.2 17.0 %copy-start.3 = (bf16[192,2560]{1,0:T(8,128)(2,1)S(1)}, bf16[192,2560]{1,0:T(8,128)(2,1)}, u32[]{:S(2)}) copy-start(bf16[192,2560]{1,0:T(8,128)(2,1)} %get-tuple-element.16.came_ref) | copy-start | bytes 2949124
  309.2 15.5 %copy-start.4 = (f32[224,2560]{1,0:T(8,128)S(1)}, f32[224,2560]{1,0:T(8,128)}, u32[]{:S(2)}) copy-start(f32[224,2560]{1,0:T(8,128)} %get-tuple-element.19) | copy-start | bytes 6881284

commit v6 on v5

--- a/solution.py
+++ b/solution.py
@@ -90,16 +90,23 @@
         pl.semaphore_signal(sem, inc=1, device_id={"tp": to}, device_id_type=pl.DeviceIdType.MESH)
 
     barrier = pltpu.get_barrier_semaphore()
-    signal(barrier, partner)
+
+    @pl.when((z != 1) | (c == 1))
+    def _():
+        signal(barrier, partner)
     for d in (0, 1):
         @pl.when((place[d] < Z - 1) & ((d == 0) | (z != 2)))
         def _():
             signal(barrier, ahead[d])
-    pl.semaphore_wait(barrier, jnp.where(z == 2, 3, 2))
+    pl.semaphore_wait(barrier, jnp.where(z == 2, 3, jnp.where((z == 1) & (c == 1), 1, 2)))
 
     @pl.when(z == 2)
     def _():
         signal(in_sem, ahead[1])
+
+    @pl.when((z == 1) & (c == 0))
+    def _():
+        signal(in_sem, partner)
 
     def own_send(d, a, h):
         return remote(arrs[a].at[half(h)], gathered[a].at[rows_of(spot(a, z + sign[d], z), c, h)],
@@ -136,7 +143,7 @@
             if d == 0:
                 @pl.when(z == 1)
                 def _():
-                    pl.semaphore_wait(in_sem, 1)
+                    pl.semaphore_wait(in_sem, 1 + c)
             for h in (0, 1):
                 own_send(d, 0, h).start()
     for h in (0, 1):

time: 326 us -> 326 us (level)
  no operation moved by 1% of the time
where the time goes in v6:
time: 326 us
  Pallas kernels  307 us (94%)
  waiting for transfers between devices  11.7 us (4%)
    pallas_call x1, Pallas kernels, line_step(): pl.pallas_call(line_kernel, out_shape=[sds((R, D), BF16), sds((R, D), BF1...  287 us
    pallas_call x1, Pallas kernels, finish_dw(): pl.pallas_call(dw_kernel, grid=(n,), out_shape=jax.ShapeDtypeStruct((D, F...  16.9 us
    ppermute x1, waiting for transfers between devices, body(): last = lax.ppermute(last, 'tp', hops[0] + hops[1])  11.7 us
  transfers between devices with their start and end apart: 2, of which 1 were waited for; matrix products, arithmetic and copies ran while one was open for 0% of the time, Pallas kernels for 6%

profile of v6, /device:TPU:0, one launch (start us, length us, event | category | flops | bytes accessed | tf_op | source)
XLA Modules:
  0.0 325.7 jit_solution(4519422659931480263)
XLA Ops:
  0.6 286.8 %shard_map.76 = (bf16[3328,2560]{1,0:T(8,128)(2,1)}, bf16[3328,2560]{1,0:T(8,128)(2,1)}, bf16[1664,1280]{1,0:T(8,128)(2,1)}, bf16[1280,2560]{1,0:T(8,128)(2,1)},...) custom-call(bf16[416,2560]{1,0:T(8,128)(2,1)} %x_ref.1, ...), custom_call_target="tpu_custom_call" | custom-call | flops 65431142400 | bytes 102236160 | tf_op jit(solution)/shard_map/pallas_call | solution.py:476
  287.4 1.3 collective-permute-start
  288.7 1.3 collective-permute-start.1
  290.0 0.0 copy-start
  290.0 2.2 copy-done
  292.2 0.0 copy-start.1
  292.2 0.0 copy-start.2
  292.2 0.0 copy-start.3
  292.2 16.9 %shard_map.78 = bf16[2560,1280]{1,0:T(8,128)(2,1)} custom-call(bf16[3328,2560]{1,0:T(8,128)(2,1)} %get-tuple-element.21.a_ref, bf16[1664,1280]{1,0:T(8,128)(2,1)S(1)} %copy-done, f32[1280,2560]{1,0:T(8,128)} %get-tuple-element.23.part_ref), custom_call_target="tpu_custom_call" | custom-call | flops 10905190400 | bytes 32440320 | tf_op jit(solution)/shard_map/pallas_call | solution.py:514
  309.2 0.0 collective-permute-done.mid_ref
  309.2 0.0 copy-done.1
  309.2 0.0 copy-done.2
  309.2 0.0 copy-done.3
  309.2 0.0 copy-start.4
  309.2 3.6 %shard_map.77 = (bf16[1280,2560]{1,0:T(8,128)(2,1)}, bf16[416,2560]{1,0:T(8,128)(2,1)}) custom-call(bf16[1280,2560]{1,0:T(8,128)(2,1)S(1)} %copy-done.1, f32[192,2560]{1,0:T(8,128)S(1)} %copy-done.2, bf16[192,2560]{1,0:T(8,128)(2,1)S(1)} %copy-done.3, bf16[128,2560]{1,0:T(8,128)(2,1)S(1)} %collective-permute-done.mid_ref), custom_call_target="tpu_custom_call" | custom-call | flops 6710886400 | bytes 13107200 | tf_op jit(solution)/shard_map/pallas_call | solution.py:544
  312.8 11.7 %collective-permute-done.1 = bf16[224,2560]{1,0:T(8,128)(2,1)S(1)} collective-permute-done((bf16[224,2560]{1,0:T(8,128)(2,1)}, bf16[224,2560]{1,0:T(8,128)(2,1)S(1)}, u32[]{:S(2)}, u32[]{:S(2)}) %collective-permute-start.1) | collective-permute-done | bytes 1146912 | tf_op jit(solution)/shard_map/ppermute | solution.py:560
  324.5 0.0 copy-done.4
  324.5 1.2 fusion
Async XLA Ops:
  287.4 21.8 %collective-permute-start = (bf16[128,2560]{1,0:T(8,128)(2,1)}, bf16[128,2560]{1,0:T(8,128)(2,1)S(1)}, u32[]{:S(2)}, u32[]{:S(2)}) collective-permute-start(bf16[128,2560]{1,0:T(8,128)(2,1)} %get-tuple-element.17), channel_id=1, source_target_pairs={{2,0},{4,6},{10,8},{12,14},{18,16},{20,22},{26,24},{28,30}} | collective-permute-start | bytes 1966088 | tf_op jit(solution)/shard_map/ppermute | solution.py:559
  288.7 35.8 %collective-permute-start.1 = (bf16[224,2560]{1,0:T(8,128)(2,1)}, bf16[224,2560]{1,0:T(8,128)(2,1)S(1)}, u32[]{:S(2)}, u32[]{:S(2)}) collective-permute-start(bf16[224,2560]{1,0:T(8,128)(2,1)} %get-tuple-element.20), channel_id=1, source_target_pairs={{2,0},{4,6},{3,1},{5,7},{10,8},{12,14},{11,9},{13,15},{18,16},{20,... | collective-permute-start | bytes 3440648 | tf_op jit(solution)/shard_map/ppermute | solution.py:560
  290.0 2.2 copy-start
  292.2 17.0 %copy-start.1 = (bf16[1280,2560]{1,0:T(8,128)(2,1)S(1)}, bf16[1280,2560]{1,0:T(8,128)(2,1)}, u32[]{:S(2)}) copy-start(bf16[1280,2560]{1,0:T(8,128)(2,1)} %get-tuple-element.14.w_ref) | copy-start | bytes 19660804
  292.2 17.0 %copy-start.2 = (f32[192,2560]{1,0:T(8,128)S(1)}, f32[192,2560]{1,0:T(8,128)}, u32[]{:S(2)}) copy-start(f32[192,2560]{1,0:T(8,128)} %get-tuple-element.15.base_ref) | copy-start | bytes 5898244
  292.2 17.0 %copy-start.3 = (bf16[192,2560]{1,0:T(8,128)(2,1)S(1)}, bf16[192,2560]{1,0:T(8,128)(2,1)}, u32[]{:S(2)}) copy-start(bf16[192,2560]{1,0:T(8,128)(2,1)} %get-tuple-element.16.came_ref) | copy-start | bytes 2949124
  309.2 15.3 %copy-start.4 = (f32[224,2560]{1,0:T(8,128)S(1)}, f32[224,2560]{1,0:T(8,128)}, u32[]{:S(2)}) copy-start(f32[224,2560]{1,0:T(8,128)} %get-tuple-element.19) | copy-start | bytes 6881284
